TPU v7x, 32 devices: a whole 2x2x4 slice. The times are simulated.
32 devices in a mesh: gx: 4 (over x, core), gy: 4 (over z), gz: 2 (over y).
Axes of the slice: x: 2, y: 2, z: 4, core: 2. Of those that a mesh axis runs over, the one named last changes fastest.
Arguments:
- right_side: float32 [16, 16, 8, 4, 256], P('gx', 'gy', 'gz'), may hold values from -80 to 80
- bond_blocks: float32 [13, 4, 4, 16, 16, 8], P(None, None, None, 'gx', 'gy', 'gz'), may hold values from -0.012 to 0.012
- bond_open: int32 [13, 16, 16, 8], P(None, 'gx', 'gy', 'gz'), may hold values 0 or 1
- onsite_blocks: float32 [4, 4, 16, 16, 8], P(None, None, 'gx', 'gy', 'gz'), may hold values from -0.012 to 0.012
- orbital_levels: float32 [4, 16, 16, 8], P(None, 'gx', 'gy', 'gz'), may hold values from 1.3 to 2.6
- column_shift: float32 [256], replicated, may hold values from 0.05 to 1
Outputs:
- solution: float32 [16, 16, 8, 4, 256], P('gx', 'gy', 'gz')
- residual: float32 [16, 16, 8, 4, 256], P('gx', 'gy', 'gz')
All inputs are finite; a program needn't handle non-finite values. No bound on the sum of `bond_open` on one device may be relied on, other than what follows from the above.
Results may differ from a plain program's by a relative error of at most 0.0003.
Values sent between devices are 32-bit elements; how exact they have to be, the bound alone decides.
A program may use at most 192 MiB of HBM per device.

v0:
```python
import functools
import itertools

import jax
import jax.numpy as jnp
import numpy as np
from jax import lax
from jax.experimental import pallas as pl
from jax.experimental.pallas import tpu as pltpu
from jax.sharding import PartitionSpec as P

ITERS = 3
LANES = 128
HALF = 64
ROWS = 8
AXES = ("gx", "gy", "gz")
MESH = pl.DeviceIdType.MESH

half_offsets = [o for o in itertools.product((-1, 0, 1), repeat=3) if o > (0, 0, 0)]
directions = [d for d in itertools.product((-1, 0, 1), repeat=3) if d != (0, 0, 0)]


def up(value, step):
    return -(-value // step) * step


class Plan:
    def __init__(self, block, orbitals, peers_along):
        self.block, self.orb = block, orbitals
        self.own = block[0] * block[1] * block[2] * orbitals
        self.base = 4 * max(block) + 8
        codes = [self.code(p) for p in itertools.product(*map(range, block)) for _ in range(orbitals)]
        self.regions, at = [], 0
        for d in directions:
            here = [{0: range(n), 1: [n], -1: [-1]}[s] for s, n in zip(d, block)]
            there = [{0: range(n), 1: [0], -1: [n - 1]}[s] for s, n in zip(d, block)]
            positions = list(itertools.product(*here))
            codes += [self.code(p) for p in positions for _ in range(orbitals)]
            pieces = []
            for slot, p in enumerate(itertools.product(*there)):
                row = ((p[0] * block[1] + p[1]) * block[2] + p[2]) * orbitals
                target = at + slot * orbitals
                if pieces and pieces[-1][0] + pieces[-1][2] == row:
                    pieces[-1][2] += orbitals
                else:
                    pieces.append([row, target, orbitals])
            rows = len(positions) * orbitals
            size = up(rows, 8)
            codes += [10**6] * (size - rows)
            self.regions.append((d, at, rows, size, pieces))
            at += size
        self.halo = at
        self.ext = up(self.own + at, LANES)
        self.halo_all = self.ext - self.own
        codes += [10**6] * (self.ext - len(codes))
        self.codes = np.array(codes, np.float32)
        nx, ny, nz = peers_along
        self.peers_along = peers_along
        self.first = [(a, 0, c) for a in range(nx) for c in range(nz) if (a, c) != (0, 0)]
        self.second = [(0, b, 0) for b in range(1, ny)]
        greet = {tuple(s % n for s, n in zip(d, peers_along)) for d in directions}
        self.greet = sorted(greet | set(self.first) | set(self.second))

    def code(self, position):
        return (position[0] * self.base + position[1]) * self.base + position[2]


def kernel(plan, rs_ref, w_ref, shift_ref, code_ref, spread_ref, sol_ref, res_ref,
           send0, recv0, sends, recvs, ext, along, a_hi, a_lo, part1, got1, part2, got2,
           hs_sem, hr_sem, s1_sem, r1_sem, s2_sem, r2_sem):
    cols = rs_ref.shape[1]
    own, orb = plan.own, plan.orb
    halo, halo_all, full = plan.halo, plan.halo_all, plan.ext
    bonds = len(half_offsets)

    def at(relative):
        return tuple(
            lax.rem(lax.axis_index(name) + (s % n), n)
            for name, s, n in zip(AXES, relative, plan.peers_along)
        )

    barrier = pltpu.get_barrier_semaphore()
    for relative in plan.greet:
        pl.semaphore_signal(barrier, inc=1, device_id=at(relative), device_id_type=MESH)

    def pack(value, send_ref, lane):
        width = value.shape[1]
        for d, start, rows, size, pieces in plan.regions:
            parts = [value[source:source + count, :] for source, target, count in pieces]
            if size > rows:
                parts.append(jnp.zeros((size - rows, width), jnp.float32))
            whole = parts[0] if len(parts) == 1 else jnp.concatenate(parts, axis=0)
            send_ref[start:start + size, lane:lane + width] = whole

    pack(rs_ref[...], send0, 0)
    pack(w_ref[...], send0, cols)
    pl.semaphore_wait(barrier, len(plan.greet))

    def halo_copies(turn, source, target):
        copies = []
        for m, (d, start, rows, size, pieces) in enumerate(plan.regions):
            copies.append(pltpu.make_async_remote_copy(
                src_ref=source.at[pl.ds(start, size)],
                dst_ref=target.at[pl.ds(start, size)],
                send_sem=hs_sem.at[turn, m],
                recv_sem=hr_sem.at[turn, m],
                device_id=at(tuple(-s for s in d)),
                device_id_type=MESH,
            ))
        return copies

    flight = halo_copies(0, send0, recv0)
    for copy in flight:
        copy.start()

    code_lane = code_ref[...][0:1, :]
    code_row = jnp.transpose(jnp.broadcast_to(code_lane, (LANES, full)))[:, 0:1]
    steps = [float(plan.code(o)) for o in half_offsets]
    lane_of = lax.broadcasted_iota(jnp.int32, (LANES, LANES), 1)

    def spread(rows_of_w):
        high = rows_of_w.astype(jnp.bfloat16).astype(jnp.float32)
        both = jnp.where(lane_of < HALF, high, rows_of_w - high).astype(jnp.bfloat16)
        return jnp.dot(both, spread_ref[...], preferred_element_type=jnp.float32)

    def placed(tiles, row_codes, lane_codes, sign, count):
        width = lane_codes.shape[1]
        blocks = []
        for g in range(0, width, LANES):
            gap = (lane_codes[:, g:g + LANES] - row_codes) * sign
            total = jnp.zeros((LANES, LANES), jnp.float32)
            for k in range(count):
                step = steps[k] if k < bonds else 0.0
                total = jnp.where(gap == step, tiles[:, k * LANES:(k + 1) * LANES], total)
            blocks.append(total)
        return jnp.concatenate(blocks, axis=1)

    ext[0:own, :] = rs_ref[...]
    forward = []
    backward = []
    for b in range(0, own, LANES):
        tiles = spread(w_ref[b:b + LANES, :])
        forward.append(placed(tiles, code_row[b:b + LANES], code_lane, 1.0, bonds + 1))
        backward.append(placed(tiles, code_row[b:b + LANES], code_lane[:, 0:own], 1.0, bonds))
    for copy in flight:
        copy.wait_recv()
    ext[own:own + halo, :] = recv0[0:halo, 0:cols]
    if own + halo < full:
        ext[own + halo:full, :] = jnp.zeros((full - own - halo, cols), jnp.float32)
        recv0[halo:halo_all, :] = jnp.zeros((halo_all - halo, cols + LANES), jnp.float32)
    for b in range(0, halo_all, LANES):
        tiles = spread(recv0[b:b + LANES, cols:cols + LANES])
        rows = code_row[own + b:own + b + LANES]
        backward.append(placed(tiles, rows, code_lane[:, 0:own], 1.0, bonds))
    for b in range(0, own, LANES):
        for g in range(0, full, LANES):
            block = forward[b // LANES][:, g:g + LANES] + jnp.transpose(backward[g // LANES][:, b:b + LANES])
            high = block.astype(jnp.bfloat16)
            a_hi[b:b + LANES, g:g + LANES] = high
            a_lo[b:b + LANES, g:g + LANES] = (block - high.astype(jnp.float32)).astype(jnp.bfloat16)

    diagonal = w_ref[...][:, (bonds + 1) * orb:(bonds + 1) * orb + 1] + shift_ref[...]

    def operate():
        vector = ext[...]
        high = vector.astype(jnp.bfloat16)
        low = (vector - high.astype(jnp.float32)).astype(jnp.bfloat16)
        total = jnp.dot(a_hi[...], low, preferred_element_type=jnp.float32)
        total = total + jnp.dot(a_lo[...], high, preferred_element_type=jnp.float32)
        total = total + jnp.dot(a_hi[...], high, preferred_element_type=jnp.float32)
        return total + diagonal * ext[0:own, :]

    pending = list(flight)

    def group(turn, members, source, target, send_sem, recv_sem):
        copies = []
        for m, relative in enumerate(members):
            copies.append(pltpu.make_async_remote_copy(
                src_ref=source.at[turn],
                dst_ref=target.at[turn, m],
                send_sem=send_sem.at[turn, m],
                recv_sem=recv_sem.at[turn, m],
                device_id=at(relative),
                device_id_type=MESH,
            ))
        for copy in copies:
            copy.start()
        pending.extend(copies)
        return copies

    for turn in range(ITERS):
        image = operate()
        mine = ext[0:own, :]
        part1[turn] = jnp.concatenate([
            jnp.sum(mine * mine, axis=0, keepdims=True),
            jnp.sum(mine * image, axis=0, keepdims=True),
            jnp.zeros((ROWS - 2, cols), jnp.float32),
        ], axis=0)
        sums = group(turn, plan.first, part1, got1, s1_sem, r1_sem)
        last = turn + 1 == ITERS
        if turn == 0:
            along[0:own, :] = image
        else:
            res_ref[...] = image
        if not last:
            pack(image, sends.at[turn], 0)
            flight = halo_copies(turn + 1, sends.at[turn], recvs.at[turn])
            for copy in flight:
                copy.start()
            pending.extend(flight)
        total = part1[turn]
        for m, copy in enumerate(sums):
            copy.wait_recv()
            total = total + got1[turn, m]
        part2[turn] = total
        sums = group(turn, plan.second, part2, got2, s2_sem, r2_sem)
        for m, copy in enumerate(sums):
            copy.wait_recv()
            total = total + got2[turn, m]
        norm, product = total[0:1], total[1:2]
        if turn == 0:
            alpha = norm / product
            direction = mine
            sol_ref[...] = alpha * mine
        else:
            ratio = norm / norm_before
            alpha = norm / (product - ratio * norm / alpha)
            direction = mine + ratio * direction
            sol_ref[...] = sol_ref[...] + alpha * direction
            along[0:own, :] = res_ref[...] + ratio * along[0:own, :]
        norm_before = norm
        if last:
            res_ref[...] = mine - alpha * along[0:own, :]
        else:
            ext[0:own, :] = mine - alpha * along[0:own, :]
            for copy in flight:
                copy.wait_recv()
            edge = recvs[turn, 0:halo, :]
            if turn > 0:
                edge = edge + ratio * along[own:own + halo, :]
            along[own:own + halo, :] = edge
            ext[own:own + halo, :] = ext[own:own + halo, :] - alpha * edge
    for copy in pending:
        copy.wait_send()


def per_device(peers_along, right_side, bond_blocks, bond_open, onsite_blocks, orbital_levels, column_shift):
    block, orb, cols = right_side.shape[:3], right_side.shape[3], right_side.shape[4]
    plan = Plan(block, orb, peers_along)
    own, bonds = plan.own, len(half_offsets)
    coupled = bond_blocks * bond_open[:, None, None].astype(jnp.float32)
    onsite_sym = 0.5 * (onsite_blocks + jnp.swapaxes(onsite_blocks, 0, 1))
    atoms = own // orb
    lines = jnp.concatenate([coupled, onsite_sym[None]], axis=0).reshape(bonds + 1, orb, orb, atoms)
    lines = jnp.transpose(lines, (3, 1, 0, 2)).reshape(own, (bonds + 1) * orb)
    levels = jnp.transpose(orbital_levels.reshape(orb, atoms)).reshape(own, 1)
    lines = jnp.concatenate([lines, levels, jnp.zeros((own, HALF - lines.shape[1] - 1), jnp.float32)], axis=1)
    lines = jnp.concatenate([lines, lines], axis=1)

    count = bonds + 1
    spread = np.zeros((2, HALF, count, LANES), np.float32)
    for k in range(count):
        for t in range(LANES):
            spread[:, k * orb + t % orb, k, t] = 1.0
    spread = jnp.asarray(spread.reshape(LANES, count * LANES), jnp.bfloat16)
    code = jnp.asarray(np.tile(plan.codes[None], (8, 1)))
    f32, bf16 = jnp.float32, jnp.bfloat16
    n1, n2, messages = len(plan.first), len(plan.second), len(directions)
    dma = pltpu.SemaphoreType.DMA
    vmem = pl.BlockSpec(memory_space=pltpu.VMEM)
    solved, left = pl.pallas_call(
        functools.partial(kernel, plan),
        out_shape=(jax.ShapeDtypeStruct((own, cols), f32),) * 2,
        in_specs=[vmem] * 5,
        out_specs=(vmem, vmem),
        scratch_shapes=[
            pltpu.VMEM((plan.halo_all + ROWS, cols + LANES), f32),
            pltpu.VMEM((plan.halo_all, cols + LANES), f32),
            pltpu.VMEM((ITERS - 1, plan.halo_all + ROWS, cols), f32),
            pltpu.VMEM((ITERS - 1, plan.halo_all, cols), f32),
            pltpu.VMEM((plan.ext, cols), f32),
            pltpu.VMEM((plan.ext, cols), f32),
            pltpu.VMEM((own, plan.ext), bf16),
            pltpu.VMEM((own, plan.ext), bf16),
            pltpu.VMEM((ITERS, ROWS, cols), f32),
            pltpu.VMEM((ITERS, n1, ROWS, cols), f32),
            pltpu.VMEM((ITERS, ROWS, cols), f32),
            pltpu.VMEM((ITERS, n2, ROWS, cols), f32),
            dma((ITERS, messages)), dma((ITERS, messages)),
            dma((ITERS, n1)), dma((ITERS, n1)),
            dma((ITERS, n2)), dma((ITERS, n2)),
        ],
        compiler_params=pltpu.CompilerParams(
            collective_id=0, has_side_effects=True, vmem_limit_bytes=60 * 1024 * 1024
        ),
    )(right_side.reshape(own, cols), lines, column_shift[None], code, spread)
    return solved.reshape(right_side.shape), left.reshape(right_side.shape)


def solution(mesh):
    field = P("gx", "gy", "gz", None, None)
    placed = (
        field,
        P(None, None, None, "gx", "gy", "gz"),
        P(None, "gx", "gy", "gz"),
        P(None, None, "gx", "gy", "gz"),
        P(None, "gx", "gy", "gz"),
        P(),
    )
    return jax.shard_map(
        functools.partial(per_device, tuple(mesh.shape[name] for name in AXES)),
        mesh=mesh,
        in_specs=placed,
        out_specs=(field, field),
        check_vma=False,
    )
```

profile of v0, /device:TPU:0, one launch (start us, length us, event | category | flops | bytes accessed | tf_op | source)
XLA Modules:
  0.0 68.2 jit_solution(15500254027024300252)
XLA Ops:
  0.6 0.8 %convert_element_type.4 = f32[13,4,4,4]{0,3,2,1:T(4,128)S(1)} convert(s32[13,4,4,4]{0,3,2,1:T(4,128)} %param.10) | non-fusion elementwise | flops 832 | bytes 6656 | tf_op jit(solution)/shard_map/convert_element_type | solution.py:251
  1.4 1.1 %broadcast_multiply_fusion = f32[13,4,4,4,2,8]{0,5,4,3,2,1:T(8,128)S(1)} fusion(f32[13,4,4,4,2,8]{0,5,4,3,2,1:T(8,128)} %bitcast.15, f32[13,4,2,8]{0,3,2,1:T(8,128)S(1)} %bitcast.16), kind=kLoop, calls=%fused_computation | loop fusion | flops 13312 | bytes 109824 | tf_op jit(solution)/shard_map/mul | solution.py:251
  2.5 0.2 copy.31
  2.7 1.0 %fusion = f32[4,4,4,4,4]{4,3,2,1,0:T(4,128)S(1)} fusion(f32[4,4,4,4,4]{4,3,2,1,0:T(4,128)} %param.11), kind=kLoop, calls=%fused_computation.2 | loop fusion | flops 2048 | bytes 8192 | tf_op jit(solution)/shard_map/mul | solution.py:252
  3.7 0.2 concatenate.14
  4.0 0.0 copy-start.1
  4.0 2.0 %copy.38 = f32[64,4,14,4]{3,2,1,0:T(8,128)S(1)} copy(f32[64,4,14,4]{0,3,1,2:T(4,128)S(1)} %maximum_bitcast_fusion) | data formatting | bytes 114688 | tf_op jit(solution)/shard_map/reshape | solution.py:255
  6.0 0.0 copy-start
  6.0 0.9 %reshape.34 = f32[256,56]{1,0:T(8,128)S(1)} reshape(f32[64,4,14,4]{3,2,1,0:T(8,128)S(1)} %copy.38) | data formatting | bytes 114688 | tf_op jit(solution)/shard_map/reshape | solution.py:255
  6.9 0.0 copy-done.1
  6.9 0.2 copy.39
  7.1 0.1 reshape.35
  7.2 0.9 %concatenate.16.w_ref = f32[256,128]{1,0:T(8,128)} concatenate(f32[256,56]{1,0:T(8,128)S(1)} %reshape.34, f32[256,1]{1,0:T(8,128)S(1)} %reshape.35, f32[256,7]{1,0:T(8,128)S(1)} %broadcast_in_dim.8, f32[256,56]{1,0:T(8,128)S(1)} %reshape.34, f32[256,1]{1,0:T(8,128)S(1)} %reshape.35, f32[256,7]{1,0:T(8,128)S(1)} %broadcast_in_dim.8), dimensions={1} | concatenate | bytes 262144 | tf_op jit(solution)/shard_map/concatenate | solution.py:258
  8.1 0.0 copy-done
  8.1 0.8 %reshape.28.rs_ref = f32[256,256]{1,0:T(8,128)} reshape(f32[4,4,4,4,256]{4,3,2,1,0:T(4,128)S(1)} %copy-done) | data formatting | bytes 524288 | tf_op jit(solution)/shard_map/reshape | solution.py:296
  8.9 55.8 %shard_map.95 = (f32[256,256]{1,0:T(8,128)}, f32[256,256]{1,0:T(8,128)}) custom-call(f32[256,256]{1,0:T(8,128)} %reshape.28.rs_ref, f32[256,128]{1,0:T(8,128)} %concatenate.16.w_ref, f32[1,256]{1,0:T(1,128)} %bitcast.18, f32[8,896]{1,0:T(8,128)} %constant.9.clone.code_ref, bf16[128,1792]{1,0:T(8,128)(2,1)} %constant.8.clone.spread_ref), custom_call_target="tpu_custom_call" | custom-call | tf_op jit(solution)/shard_map/pallas_call | solution.py:271
  64.7 1.7 %reshape.32 = f32[4,4,4,4,256]{4,3,2,1,0:T(4,128)} reshape(f32[256,256]{1,0:T(8,128)} %get-tuple-element.4) | data formatting | bytes 524288 | tf_op jit(solution)/shard_map/reshape | solution.py:297
  66.4 1.7 %reshape.33 = f32[4,4,4,4,256]{4,3,2,1,0:T(4,128)} reshape(f32[256,256]{1,0:T(8,128)} %get-tuple-element.5) | data formatting | bytes 524288 | tf_op jit(solution)/shard_map/reshape | solution.py:297
  (2 shorter events, 0.0 us)
Async XLA Ops:
  4.0 2.9 %copy-start.1 = (f32[4,4,4,4]{3,2,1,0:T(4,128)S(1)}, f32[4,4,4,4]{3,2,1,0:T(4,128)}, u32[]{:S(2)}) copy-start(f32[4,4,4,4]{3,2,1,0:T(4,128)} %param.12) | copy-start | bytes 3076
  6.0 2.1 %copy-start = (f32[4,4,4,4,256]{4,3,2,1,0:T(4,128)S(1)}, f32[4,4,4,4,256]{4,3,2,1,0:T(4,128)}, u32[]{:S(2)}) copy-start(f32[4,4,4,4,256]{4,3,2,1,0:T(4,128)} %param.8) | copy-start | bytes 786436
where the time goes:
time: 68.5 us; the launch traced here: 68.2 us
  Pallas kernels  55.8 us (81%)
  local copies, waits for them, and re-layouts  8.73 us (13%)
  other arithmetic  2.92 us (4%)
  between operations  0.71 us (1%)
    pallas_call x1, Pallas kernels, per_device(): pl.pallas_call(functools.partial(kernel, plan), out_shape=(jax.ShapeDtype...  55.8 us
    reshape x2, local copies, waits for them, and re-layouts, per_device(): return (solved.reshape(right_side.shape), left.reshape(right_side.shape))  3.45 us
    reshape x2, local copies, waits for them, and re-layouts, per_device(): lines = jnp.transpose(lines, (3, 1, 0, 2)).reshape(own, (bonds + 1) * orb)  2.9 us

commit v1 on v0

v1 whole, which is shorter than its diff:
```python
import functools
import itertools

import jax
import jax.numpy as jnp
from jax import lax
from jax.experimental import pallas as pl
from jax.experimental.pallas import tpu as pltpu
from jax.sharding import PartitionSpec as P

ITERS = 3
LANES = 128
ROWS = 8
AXES = ("gx", "gy", "gz")
MESH = pl.DeviceIdType.MESH

bonds = [o for o in itertools.product((-1, 0, 1), repeat=3) if o > (0, 0, 0)]
NB = len(bonds)
ahead_runs = [(1, 3), (10, 3)]
behind_runs = [(4, 3)]
assert all(bonds[k][1] == 1 for at, n in ahead_runs for k in range(at, at + n))
assert all(bonds[k][1] == -1 for at, n in behind_runs for k in range(at, at + n))


class Plan:
    def __init__(self, block, orb, cols, peers):
        self.X, self.Y, self.Z = block
        self.O, self.cols = orb, cols
        self.nx, self.ny, self.nz = peers
        self.S = self.nx * self.nz
        self.l = self.X * self.Z
        self.L = self.S * self.l
        self.G = LANES // self.l
        self.Cw = cols // self.S
        self.YO = self.Y * orb
        self.HL = self.YO * self.l
        self.HT = self.HL // LANES
        self.H = cols // LANES
        self.JT = LANES // (self.Y * self.l)
        self.tiles = orb * orb // self.JT
        self.CR = (NB + 1) * self.tiles
        self.OC = orb * self.Cw
        assert self.tiles == ROWS and self.S % self.G == 0 and self.Cw % ROWS == 0


def kernel(plan, rs_hbm, bb_hbm, open_ref, onsite_ref, level_ref, shift_ref, sol_hbm, res_hbm,
           RS, BB, T, RB, CS, CR, M, MB, V, VS, SB, YB, MG, TG, WQ, OS,
           in_sem, a_s, a_r, c_s, c_r, hv_s, hv_r, hm_s, hm_r, th_s, th_r, y_s, y_r, mo_s, mo_r, w_s, w_r):
    p = plan
    X, Y, Z, O, S, L, l, G, Cw, H, OC = p.X, p.Y, p.Z, p.O, p.S, p.L, p.l, p.G, p.Cw, p.H, p.OC
    f32 = jnp.float32
    ax, ay, az = (lax.axis_index(name) for name in AXES)
    me = ax * p.nz + az
    pending = []

    def mate(r):
        d = lax.rem(me + r, S)
        return d, (lax.div(d, p.nz), ay, lax.rem(d, p.nz))

    def source(r):
        return lax.rem(me + (S - r), S)

    def along(r):
        return (ax, lax.rem(ay + (r % p.ny), p.ny), az)

    def send(src, dst, ssem, rsem, device):
        copy = pltpu.make_async_remote_copy(
            src_ref=src, dst_ref=dst, send_sem=ssem, recv_sem=rsem, device_id=device, device_id_type=MESH
        )
        copy.start()
        pending.append(copy)
        return copy

    loads = []
    for x in range(X):
        for y in range(Y):
            n = Z * H * O
            copy = pltpu.make_async_copy(
                rs_hbm.at[x, y], RS.at[pl.ds((y * X + x) * n, n)], in_sem.at[x * Y + y])
            copy.start()
            loads.append(copy)
    bond_load = pltpu.make_async_copy(bb_hbm, BB, in_sem.at[X * Y])
    bond_load.start()

    barrier = pltpu.get_barrier_semaphore()
    for r in range(1, S):
        pl.semaphore_signal(barrier, inc=1, device_id=mate(r)[1], device_id_type=MESH)
    for r in range(1, p.ny):
        pl.semaphore_signal(barrier, inc=1, device_id=along(r), device_id_type=MESH)

    lane = lax.broadcasted_iota(jnp.int32, (1, L), 1)
    lane128 = lax.broadcasted_iota(jnp.int32, (1, LANES), 1)

    def roll(v, by):
        by = by % v.shape[1]
        return v if by == 0 else pltpu.roll(v, by, 1)

    zl = lane & (Z - 1)
    xl = (lane // Z) & (X - 1)
    gz = (lane // l) & (p.nz - 1)

    def shift_z(v, s):
        if s == 0:
            return v
        edge, outer = (zl == Z - 1, gz == p.nz - 1) if s > 0 else (zl == 0, gz == 0)
        far = l - (Z - 1)
        out = jnp.where(edge, roll(v, -s * far), roll(v, -s))
        return jnp.where(edge & outer, roll(v, -s * (far - p.nz * l)), out)

    def shift_x(v, s):
        if s == 0:
            return v
        edge = (xl == X - 1) if s > 0 else (xl == 0)
        far = p.nz * l - (X - 1) * Z
        return jnp.where(edge, roll(v, -s * far), roll(v, -s * Z))

    block_of = lane128 // l

    def butterfly(arrays):
        arrays = list(arrays)
        m = 1
        while m < G:
            low = (block_of & m) == 0
            for a in range(G):
                if a & m == 0:
                    b = a | m
                    first, second = arrays[a], arrays[b]
                    arrays[a] = jnp.where(low, first, roll(second, m * l))
                    arrays[b] = jnp.where(low, roll(first, -m * l), second)
            m *= 2
        return arrays

    for copy in loads:
        copy.wait()
    step = H * O
    for h in range(H):
        rows = jnp.concatenate([
            RS[pl.ds(y * X * Z * step + h * O + o, l, stride=step), :] for y in range(Y) for o in range(O)
        ], axis=0)
        T[h * LANES:(h + 1) * LANES, :] = jnp.transpose(rows)
    pl.semaphore_wait(barrier, S - 1 + p.ny - 1)
    field_copies = []
    for r in range(1, S):
        d, device = mate(r)
        field_copies.append(send(
            T.at[pl.ds(pl.multiple_of(d * Cw, ROWS), Cw)], RB.at[me], a_s.at[r - 1], a_r.at[r - 1], device))
    RB[me] = T[pl.ds(pl.multiple_of(me * Cw, ROWS), Cw), :]

    def spread_z(block):
        n = block.shape[0]
        out = jnp.zeros((n, LANES), f32)
        for z in range(Z):
            out = jnp.where((lane128 & (Z - 1)) == z, block[:, z:z + 1], out)
        row = lax.broadcasted_iota(jnp.int32, (n, LANES), 0)
        col = lax.broadcasted_iota(jnp.int32, (n, LANES), 1)
        x_row, y_row = (row // Y) & (X - 1), row & (Y - 1)
        x_col, y_col = (col // Z) & (X - 1), (col // l) & (Y - 1)
        return jnp.where((x_row == x_col) & (y_row == y_col), out, 0.0)

    onsite = spread_z(onsite_ref[...])
    level = spread_z(level_ref[...])
    XY = X * Y
    pair = [jnp.sum(onsite[n * XY:(n + 1) * XY], axis=0, keepdims=True) for n in range(O * O)]
    diagonal = [jnp.sum(level[n * XY:(n + 1) * XY], axis=0, keepdims=True) for n in range(O)]
    j_low = lane128 // (Y * l)
    for i in range(O):
        for jh in range(O // p.JT):
            line = jnp.zeros((1, LANES), f32)
            for jl in range(p.JT):
                j = jh * p.JT + jl
                term = 0.5 * (pair[i * O + j] + pair[j * O + i])
                if i == j:
                    term = term + diagonal[i]
                line = jnp.where(j_low == jl, term, line)
            row = NB * ROWS + i * (O // p.JT) + jh
            CS[row:row + 1, :] = line

    bond_load.wait()
    is_open = open_ref[...].astype(f32)
    is_open = jnp.concatenate([is_open] * p.JT, axis=0)
    x_of, y_of = (lane128 // (Y * Z)) & (X - 1), (lane128 // Z) & (Y - 1)
    x_to, y_to = (lane128 // Z) & (X - 1), (lane128 // (X * Z)) & (Y - 1)
    source_lane = (lane128 & (Z - 1)) + x_to * (Y * Z) + y_to * Z + j_low * (Y * l)
    gaps = sorted({(x * Y * Z + y * Z) - (y * X * Z + x * Z) for x in range(X) for y in range(Y)})
    for t in range(p.tiles):
        block = BB[t * LANES:(t + 1) * LANES, :] * is_open
        block = jnp.concatenate([block, jnp.zeros((LANES, LANES - NB), f32)], axis=1)
        block = jnp.transpose(block)[0:2 * ROWS, :]
        out = block
        for gap in gaps:
            if gap:
                out = jnp.where(source_lane - lane128 == gap, roll(block, -gap), out)
        CS[pl.ds(t, NB, stride=ROWS), :] = out[0:NB, :]
    coef_copies = []
    for r in range(1, S):
        d, device = mate(r)
        coef_copies.append(send(CS, CR.at[me], c_s.at[r - 1], c_r.at[r - 1], device))
    CR[me] = CS[...]

    def halo_field(m):
        return [
            send(V.at[m, 1], V.at[m, Y + 1], hv_s.at[m, 0], hv_r.at[m, 0], along(-1)),
            send(V.at[m, Y], V.at[m, 0], hv_s.at[m, 1], hv_r.at[m, 1], along(1)),
        ]

    def arrived(copies):
        for copy in copies:
            copy.wait_recv()

    arrived(field_copies)
    for t in range(p.HT):
        for first in range(0, S, G):
            blocks = butterfly([RB[first + n, :, t * LANES:(t + 1) * LANES] for n in range(G)])
            at = first // G * LANES
            for n in range(G):
                y, o = divmod(t * G + n, O)
                V[0, y + 1, o * Cw:(o + 1) * Cw, at:at + LANES] = blocks[n]
    halo = halo_field(0)

    arrived(coef_copies)
    for first in range(0, S, G):
        blocks = butterfly([CR[first + n] for n in range(G)])
        at = first // G * LANES
        for n in range(G):
            jl, y = divmod(n, Y)
            M[jl, y + 1, :, at:at + LANES] = blocks[n]
    coef_halo = []
    for n, (run, y_from, y_to_slot, way) in enumerate(
            [(run, Y, 0, 1) for run in ahead_runs] + [(run, 1, Y + 1, -1) for run in behind_runs]):
        rows = pl.ds(run[0] * ROWS, run[1] * ROWS)
        coef_halo.append(send(
            M.at[:, y_from, rows], M.at[:, y_to_slot, rows], hm_s.at[n], hm_r.at[n], along(way)))

    HALFJ = O // p.JT
    diag_rows = [(i % p.JT, NB * ROWS + i * HALFJ + i // p.JT) for i in range(O)]
    part = jnp.zeros((1, L), f32)
    for y in range(1, Y + 1):
        for jl, row in diag_rows:
            part = part + M[jl, y, row:row + 1, :]
    TG[ay] = jnp.broadcast_to(jnp.sum(part, axis=1, keepdims=True), (ROWS, LANES))
    theta_copies = [
        send(TG.at[ay], TG.at[ay], th_s.at[r - 1], th_r.at[r - 1], along(r)) for r in range(1, p.ny)]

    def mirror(k, y):
        o = bonds[k]
        for jl in range(p.JT):
            block = M[jl, y + 1 - o[1], k * ROWS:(k + 1) * ROWS, :]
            MB[k, jl, y] = shift_x(shift_z(block, -o[2]), -o[0])

    def inside(y):
        return 0 <= y < Y

    for k in range(NB):
        for y in range(Y):
            if inside(y - bonds[k][1]):
                mirror(k, y)

    def place(sx, sz):
        n = (sx + 1) * 3 + sz + 1
        return n - (n > 4)

    def spread_field(m, slot):
        for o in range(O):
            rows = slice(o * Cw, (o + 1) * Cw)
            base = V[m, slot, rows, :]
            for sz in (-1, 0, 1):
                turned = shift_z(base, sz)
                for sx in (-1, 0, 1):
                    if (sx, sz) != (0, 0):
                        VS[place(sx, sz), slot, rows, :] = shift_x(turned, sx)

    def add_bonds(acc, m, y, steps):
        for k, o in enumerate(bonds):
            for sign in (1, -1):
                if sign * o[1] not in steps:
                    continue
                slot = y + 1 + sign * o[1]
                sx, sz = sign * o[0], sign * o[2]
                for j in range(O):
                    rows = slice(j * Cw, (j + 1) * Cw)
                    v = V[m, slot, rows, :] if (sx, sz) == (0, 0) else VS[place(sx, sz), slot, rows, :]
                    for i in range(O):
                        if sign > 0:
                            row = k * ROWS + i * HALFJ + j // p.JT
                            c = M[j % p.JT, y + 1, row:row + 1, :]
                        else:
                            row = j * HALFJ + i // p.JT
                            c = MB[k, i % p.JT, y, row:row + 1, :]
                        acc[i] = acc[i] + c * v

    def add_onsite(acc, m, y, theta):
        for j in range(O):
            v = V[m, y + 1, j * Cw:(j + 1) * Cw, :]
            for i in range(O):
                row = NB * ROWS + i * HALFJ + j // p.JT
                c = M[j % p.JT, y + 1, row:row + 1, :]
                if i == j:
                    c = c - theta
                acc[i] = acc[i] + c * v

    def put(acc, m, y):
        for i in range(O):
            V[m, y + 1, i * Cw:(i + 1) * Cw, :] = acc[i]

    def take(m, y):
        return [V[m, y + 1, i * Cw:(i + 1) * Cw, :] for i in range(O)]

    def zeros():
        return [jnp.zeros((Cw, L), f32) for _ in range(O)]

    def moment(a, b):
        total = jnp.zeros((Cw, L), f32)
        for y in range(Y):
            for i in range(O):
                rows = slice(i * Cw, (i + 1) * Cw)
                total = total + V[a, y + 1, rows, :] * V[b, y + 1, rows, :]
        return jnp.sum(total, axis=1, keepdims=True)

    moments = []
    home_copies = []

    def go_home(m):
        for t in range(p.HT):
            for first in range(0, S, G):
                at = first // G * LANES
                blocks = []
                for n in range(G):
                    y, o = divmod(t * G + n, O)
                    blocks.append(V[m, y + 1, o * Cw:(o + 1) * Cw, at:at + LANES])
                blocks = butterfly(blocks)
                for n in range(G):
                    SB[m - 1, first + n, :, t * LANES:(t + 1) * LANES] = blocks[n]
        mine = pl.ds(pl.multiple_of(me * Cw, ROWS), Cw)
        for r in range(1, S):
            d, device = mate(r)
            home_copies.append(send(
                SB.at[m - 1, d], YB.at[m - 1, mine], y_s.at[m - 1, r - 1], y_r.at[m - 1, r - 1], device))
        YB[m - 1, mine] = SB[m - 1, me]

    theta = None
    for m in range(ITERS):
        for slot in range(1, Y + 1):
            spread_field(m, slot)
        for y in range(Y):
            acc = zeros()
            add_bonds(acc, m, y, [s for s in (-1, 0, 1) if inside(y + s)])
            put(acc, m + 1, y)
        if m == 0:
            moments.append(moment(0, 0))
            arrived(theta_copies)
            theta = TG[0][0:1, 0:1]
            for n in range(1, p.ny):
                theta = theta + TG[n][0:1, 0:1]
            theta = theta * (1.0 / (p.ny * Y * L * O))
        arrived(halo)
        if m == 0:
            arrived(coef_halo)
            for k in range(NB):
                for y in range(Y):
                    if not inside(y - bonds[k][1]):
                        mirror(k, y)
        for slot, y, s in ((0, 0, -1), (Y + 1, Y - 1, 1)):
            spread_field(m, slot)
            acc = take(m + 1, y)
            add_bonds(acc, m, y, [s])
            add_onsite(acc, m, y, theta)
            put(acc, m + 1, y)
        if m + 1 < ITERS:
            halo = halo_field(m + 1)
        for y in range(1, Y - 1):
            acc = take(m + 1, y)
            add_onsite(acc, m, y, theta)
            put(acc, m + 1, y)
        go_home(m + 1)
        moments.append(moment(m, m + 1))
        if m + 1 < ITERS:
            moments.append(moment(m + 1, m + 1))

    table = jnp.zeros((Cw, LANES), f32)
    for n, value in enumerate(moments):
        table = jnp.where(lane128 == n, value, table)
    if Cw < LANES:
        table = jnp.concatenate([table, jnp.zeros((LANES - Cw, LANES), f32)], axis=0)
    MG[ay] = jnp.transpose(table)[0:ROWS, :]
    arrived([send(MG.at[ay], MG.at[ay], mo_s.at[r - 1], mo_r.at[r - 1], along(r)) for r in range(1, p.ny)])
    total = MG[0]
    for n in range(1, p.ny):
        total = total + MG[n]
    m_of = [total[n:n + 1, :] for n in range(2 * ITERS)]
    shift = jnp.zeros((1, LANES), f32)
    for d in range(S):
        h, at = divmod(d * Cw, LANES)
        shift = jnp.where(me == d, roll(shift_ref[:, h * LANES:(h + 1) * LANES], -at), shift)
    shift = shift + theta

    def inner(u, v):
        out = None
        for a, first in enumerate(u):
            for b, second in enumerate(v):
                term = first * second * m_of[a + b]
                out = term if out is None else out + term
        return out

    def plus(u, v, factor):
        n = max(len(u), len(v))
        out = []
        for a in range(n):
            if a < len(v):
                term = factor * v[a]
                out.append(u[a] + term if a < len(u) else term)
            else:
                out.append(u[a])
        return out

    one = jnp.ones((1, LANES), f32)
    answer, residual, direction, norm = [], [one], [one], m_of[0]
    for turn in range(ITERS):
        image = [shift * direction[0]]
        for a in range(1, len(direction)):
            image.append(direction[a - 1] + shift * direction[a])
        image.append(direction[-1])
        alpha = norm / inner(direction, image)
        answer = plus(answer, direction, alpha)
        residual = plus(residual, image, -alpha)
        if turn + 1 < ITERS:
            fresh = inner(residual, residual)
            direction = plus(residual, direction, fresh / norm)
            norm = fresh
    factors = answer + residual
    WQ[me] = jnp.concatenate(factors + [jnp.zeros((ROWS - len(factors), LANES), f32)], axis=0)
    factor_copies = []
    for r in range(1, S):
        d, device = mate(r)
        factor_copies.append(send(WQ.at[me], WQ.at[me], w_s.at[r - 1], w_r.at[r - 1], device))
    arrived(factor_copies)
    arrived(home_copies)

    outs = []
    for h in range(H):
        lines = jnp.zeros((ROWS, LANES), f32)
        per = LANES // Cw
        for n in range(per):
            d = h * per + n
            lines = jnp.where(lane128 // Cw == n, roll(WQ[d], n * Cw), lines)
        column = jnp.transpose(lines)
        rows = slice(h * LANES, (h + 1) * LANES)
        basis = [T[rows, :]] + [YB[n, rows, :] for n in range(ITERS)]
        for which, hbm in ((0, sol_hbm), (1, res_hbm)):
            at = which * ITERS
            field = column[:, at:at + 1] * basis[0]
            for n in range(1, ITERS + which):
                field = field + column[:, at + n:at + n + 1] * basis[n]
            field = jnp.transpose(field)
            for y in range(Y):
                for o in range(O):
                    n = (y * O + o) * l
                    OS[which, pl.ds(y * X * Z * step + h * O + o, l, stride=step), :] = field[n:n + l, :]
    for which, hbm in ((0, sol_hbm), (1, res_hbm)):
        for x in range(X):
            for y in range(Y):
                n = Z * H * O
                copy = pltpu.make_async_copy(
                    OS.at[which, pl.ds((y * X + x) * n, n)], hbm.at[x, y], in_sem.at[(which * X + x) * Y + y])
                copy.start()
                outs.append(copy)
    for copy in outs:
        copy.wait()
    for copy in pending:
        copy.wait_send()


def per_device(peers, right_side, bond_blocks, bond_open, onsite_blocks, orbital_levels, column_shift):
    block, orb, cols = right_side.shape[:3], right_side.shape[3], right_side.shape[4]
    p = Plan(block, orb, cols, peers)
    X, Y, Z, O, S, L, H = p.X, p.Y, p.Z, p.O, p.S, p.L, p.H
    f32 = jnp.float32
    right = right_side.reshape(X, Y, Z, O, H, LANES).transpose(0, 1, 2, 4, 3, 5).reshape(X, Y, Z * H * O, LANES)
    blocks = jnp.transpose(bond_blocks, (1, 2, 3, 4, 5, 0)).reshape(O * O * X * Y * Z, NB)
    opened = jnp.transpose(bond_open, (1, 2, 3, 0)).reshape(X * Y * Z, NB)
    onsite = onsite_blocks.reshape(O * O * X * Y, Z)
    levels = orbital_levels.reshape(O * X * Y, Z)
    dma = pltpu.SemaphoreType.DMA
    vmem, anywhere = pl.BlockSpec(memory_space=pltpu.VMEM), pl.BlockSpec(memory_space=pl.ANY)

    def scratch(*shape):
        return pltpu.VMEM(shape, f32)

    outs = pl.pallas_call(
        functools.partial(kernel, p),
        out_shape=(jax.ShapeDtypeStruct(right.shape, f32),) * 2,
        in_specs=[anywhere, anywhere] + [vmem] * 4,
        out_specs=(anywhere, anywhere),
        scratch_shapes=[
            scratch(X * Y * Z * H * O, LANES),
            scratch(O * O * X * Y * Z, NB),
            scratch(cols, p.HL),
            scratch(S, p.Cw, p.HL),
            scratch(p.CR, LANES),
            scratch(S, p.CR, LANES),
            scratch(p.JT, Y + 2, p.CR, L),
            scratch(NB, p.JT, Y, ROWS, L),
            scratch(ITERS + 1, Y + 2, p.OC, L),
            scratch(8, Y + 2, p.OC, L),
            scratch(ITERS, S, p.Cw, p.HL),
            scratch(ITERS, cols, p.HL),
            scratch(p.ny, ROWS, LANES),
            scratch(p.ny, ROWS, LANES),
            scratch(S, ROWS, LANES),
            scratch(2, X * Y * Z * H * O, LANES),
            dma((2 * X * Y,)),
            dma((S - 1,)), dma((S - 1,)), dma((S - 1,)), dma((S - 1,)),
            dma((ITERS, 2)), dma((ITERS, 2)), dma((3,)), dma((3,)),
            dma((p.ny - 1,)), dma((p.ny - 1,)),
            dma((ITERS, S - 1)), dma((ITERS, S - 1)),
            dma((p.ny - 1,)), dma((p.ny - 1,)), dma((S - 1,)), dma((S - 1,)),
        ],
        compiler_params=pltpu.CompilerParams(
            collective_id=0, has_side_effects=True, vmem_limit_bytes=60 * 1024 * 1024
        ),
    )(right, blocks, opened, onsite, levels, column_shift[None])

    def back(v):
        return v.reshape(X, Y, Z, H, O, LANES).transpose(0, 1, 2, 4, 3, 5).reshape(right_side.shape)

    return back(outs[0]), back(outs[1])


def solution(mesh):
    field = P("gx", "gy", "gz", None, None)
    placed = (
        field,
        P(None, None, None, "gx", "gy", "gz"),
        P(None, "gx", "gy", "gz"),
        P(None, None, "gx", "gy", "gz"),
        P(None, "gx", "gy", "gz"),
        P(),
    )
    return jax.shard_map(
        functools.partial(per_device, tuple(mesh.shape[name] for name in AXES)),
        mesh=mesh,
        in_specs=placed,
        out_specs=(field, field),
        check_vma=False,
    )
```

time: 68.5 us -> 52.2 us (0.76)
  Pallas kernels: 55.8 us -> 48.9 us
  local copies, waits for them, and re-layouts: 8.73 us -> 2.42 us
  other arithmetic: 2.92 us -> 0 us
    reshape x7 -> x0, local copies, waits for them, and re-layouts: 7.43 us -> none  [the longest x2 3.45 us: per_device(): return (solved.reshape(right_side.shape), left.reshape(right_side.shape))]
    pallas_call x1, Pallas kernels: 55.8 us -> 48.9 us  [per_device(): pl.pallas_call(functools.partial(kernel, p), out_shape=(jax.ShapeDtypeStr...]
    unnamed x4, local copies, waits for them, and re-layouts: 0.01 us -> 2.42 us
    mul x2 -> x0, other arithmetic: 2.12 us -> none  [the longest x1 1.08 us: per_device(): coupled = bond_blocks * bond_open[:, None, None].astype(jnp.float32)]
    concatenate x3 -> x0, local copies, waits for them, and re-layouts: 1.28 us -> none  [the longest x1 0.89 us: per_device(): lines = jnp.concatenate([lines, lines], axis=1)]
    convert_element_type x1 -> x0, other arithmetic: 0.77 us -> none  [per_device(): coupled = bond_blocks * bond_open[:, None, None].astype(jnp.float32)]
where the time goes in v1:
time: 52.2 us; the launch traced here: 52 us
  Pallas kernels  48.9 us (94%)
  local copies, waits for them, and re-layouts  2.42 us (5%)
  between operations  0.65 us (1%)
    pallas_call x1, Pallas kernels, per_device(): pl.pallas_call(functools.partial(kernel, p), out_shape=(jax.ShapeDtypeStr...  48.9 us
    unnamed x4, local copies, waits for them, and re-layouts  2.42 us

profile of v1, /device:TPU:0, one launch (start us, length us, event | category | flops | bytes accessed | tf_op | source)
XLA Modules:
  0.0 52.0 jit_solution(14332169747739969302)
XLA Ops:
  0.6 48.9 %shard_map.77 = (f32[4,4,32,128]{3,2,1,0:T(8,128)}, f32[4,4,32,128]{3,2,1,0:T(8,128)}) custom-call(f32[4,4,32,128]{3,2,1,0:T(8,128)} %bitcast.25, f32[1024,13]{1,0:T(8,128)} %bitcast.24, s32[64,13]{1,0:T(8,128)} %bitcast.29, f32[256,4]{1,0:T(8,128)} %bitcast.28, f32[64,4]{1,0:T(8,128)} %bitcast.30, f32[1,256]{1,0:T(1,128)} %bitcast.31), custom_call_target="tpu_custom_call" | custom-call | tf_op jit(solution)/shard_map/pallas_call | solution.py:488
  49.6 0.0 copy-start
  49.6 1.7 %copy.13 = f32[4,4,4,4,256]{4,3,2,1,0:T(4,128)} copy(f32[4,4,4,4,256]{4,3,2,1,0:T(4,128)} %bitcast.27) | data formatting | bytes 524288
  51.3 0.0 copy-done
  51.3 0.7 %copy.14 = f32[4,4,4,4,256]{4,3,2,1,0:T(4,128)} copy(f32[4,4,4,4,256]{4,3,2,1,0:T(4,128)S(1)} %bitcast.26) | data formatting | bytes 524288
Async XLA Ops:
  49.6 1.7 %copy-start = (f32[4,4,32,128]{3,2,1,0:T(8,128)S(1)}, f32[4,4,32,128]{3,2,1,0:T(8,128)}, u32[]{:S(2)}) copy-start(f32[4,4,32,128]{3,2,1,0:T(8,128)} %get-tuple-element.5) | copy-start | bytes 786436

commit v2 on v1

--- a/solution.py
+++ b/solution.py
@@ -43,8 +43,8 @@
         assert self.tiles == ROWS and self.S % self.G == 0 and self.Cw % ROWS == 0
 
 
-def kernel(plan, rs_hbm, bb_hbm, open_ref, onsite_ref, level_ref, shift_ref, sol_hbm, res_hbm,
-           RS, BB, T, RB, CS, CR, M, MB, V, VS, SB, YB, MG, TG, WQ, OS,
+def kernel(plan, rs_hbm, bb_hbm, open_hbm, onsite_hbm, level_hbm, shift_hbm, sol_hbm, res_hbm,
+           RS, BB, open_ref, onsite_ref, level_ref, shift_ref, PM, LH, T, RB, CS, CR, M, MB, V, VS, SB, YB, MG, TG, WQ, OS,
            in_sem, a_s, a_r, c_s, c_r, hv_s, hv_r, hm_s, hm_r, th_s, th_r, y_s, y_r, mo_s, mo_r, w_s, w_r):
     p = plan
     X, Y, Z, O, S, L, l, G, Cw, H, OC = p.X, p.Y, p.Z, p.O, p.S, p.L, p.l, p.G, p.Cw, p.H, p.OC
@@ -70,6 +70,12 @@
         copy.start()
         pending.append(copy)
         return copy
+
+    barrier = pltpu.get_barrier_semaphore()
+    for r in range(1, S):
+        pl.semaphore_signal(barrier, inc=1, device_id=mate(r)[1], device_id_type=MESH)
+    for r in range(1, p.ny):
+        pl.semaphore_signal(barrier, inc=1, device_id=along(r), device_id_type=MESH)
 
     loads = []
     for x in range(X):
@@ -79,14 +85,12 @@
                 rs_hbm.at[x, y], RS.at[pl.ds((y * X + x) * n, n)], in_sem.at[x * Y + y])
             copy.start()
             loads.append(copy)
-    bond_load = pltpu.make_async_copy(bb_hbm, BB, in_sem.at[X * Y])
-    bond_load.start()
-
-    barrier = pltpu.get_barrier_semaphore()
-    for r in range(1, S):
-        pl.semaphore_signal(barrier, inc=1, device_id=mate(r)[1], device_id_type=MESH)
-    for r in range(1, p.ny):
-        pl.semaphore_signal(barrier, inc=1, device_id=along(r), device_id_type=MESH)
+    small_loads = []
+    for n, (src, dst) in enumerate(((onsite_hbm, onsite_ref), (level_hbm, level_ref), (bb_hbm, BB),
+                                    (open_hbm, open_ref), (shift_hbm, shift_ref))):
+        copy = pltpu.make_async_copy(src, dst, in_sem.at[X * Y + n])
+        copy.start()
+        small_loads.append(copy)
 
     lane = lax.broadcasted_iota(jnp.int32, (1, L), 1)
     lane128 = lax.broadcasted_iota(jnp.int32, (1, LANES), 1)
@@ -95,24 +99,30 @@
         by = by % v.shape[1]
         return v if by == 0 else pltpu.roll(v, by, 1)
 
-    zl = lane & (Z - 1)
-    xl = (lane // Z) & (X - 1)
-    gz = (lane // l) & (p.nz - 1)
-
-    def shift_z(v, s):
-        if s == 0:
-            return v
-        edge, outer = (zl == Z - 1, gz == p.nz - 1) if s > 0 else (zl == 0, gz == 0)
-        far = l - (Z - 1)
-        out = jnp.where(edge, roll(v, -s * far), roll(v, -s))
-        return jnp.where(edge & outer, roll(v, -s * (far - p.nz * l)), out)
-
-    def shift_x(v, s):
-        if s == 0:
-            return v
-        edge = (xl == X - 1) if s > 0 else (xl == 0)
-        far = p.nz * l - (X - 1) * Z
-        return jnp.where(edge, roll(v, -s * far), roll(v, -s * Z))
+    zg = ((lane // l) & (p.nz - 1)) * Z + (lane & (Z - 1))
+    xg = (lane // (l * p.nz)) * X + ((lane // Z) & (X - 1))
+    row_of = lax.broadcasted_iota(jnp.int32, (L, L), 0)
+
+    def place(sx, sz):
+        n = (sx + 1) * 3 + sz + 1
+        return n - (n > 4)
+
+    def make_shifts():
+        for sx in (-1, 0, 1):
+            for sz in (-1, 0, 1):
+                if (sx, sz) == (0, 0):
+                    continue
+                x_to, z_to = (xg + sx) & (p.nx * X - 1), (zg + sz) & (p.nz * Z - 1)
+                from_lane = ((x_to // X) * p.nz + z_to // Z) * l + (x_to & (X - 1)) * Z + (z_to & (Z - 1))
+                matrix = jnp.where(row_of == from_lane, 1.0, 0.0).astype(jnp.bfloat16)
+                at = place(sx, sz) * L
+                PM[0:L, at:at + L] = matrix
+                PM[L:2 * L, at:at + L] = matrix
+
+    def halves(v):
+        high = v.astype(jnp.bfloat16)
+        low = (v - high.astype(f32)).astype(jnp.bfloat16)
+        return jnp.concatenate([high, low], axis=1)
 
     block_of = lane128 // l
 
@@ -138,6 +148,7 @@
             RS[pl.ds(y * X * Z * step + h * O + o, l, stride=step), :] for y in range(Y) for o in range(O)
         ], axis=0)
         T[h * LANES:(h + 1) * LANES, :] = jnp.transpose(rows)
+    make_shifts()
     pl.semaphore_wait(barrier, S - 1 + p.ny - 1)
     field_copies = []
     for r in range(1, S):
@@ -157,6 +168,8 @@
         x_col, y_col = (col // Z) & (X - 1), (col // l) & (Y - 1)
         return jnp.where((x_row == x_col) & (y_row == y_col), out, 0.0)
 
+    for copy in small_loads[0:2]:
+        copy.wait()
     onsite = spread_z(onsite_ref[...])
     level = spread_z(level_ref[...])
     XY = X * Y
@@ -175,7 +188,8 @@
             row = NB * ROWS + i * (O // p.JT) + jh
             CS[row:row + 1, :] = line
 
-    bond_load.wait()
+    for copy in small_loads[2:]:
+        copy.wait()
     is_open = open_ref[...].astype(f32)
     is_open = jnp.concatenate([is_open] * p.JT, axis=0)
     x_of, y_of = (lane128 // (Y * Z)) & (X - 1), (lane128 // Z) & (Y - 1)
@@ -241,33 +255,35 @@
     theta_copies = [
         send(TG.at[ay], TG.at[ay], th_s.at[r - 1], th_r.at[r - 1], along(r)) for r in range(1, p.ny)]
 
-    def mirror(k, y):
-        o = bonds[k]
-        for jl in range(p.JT):
-            block = M[jl, y + 1 - o[1], k * ROWS:(k + 1) * ROWS, :]
-            MB[k, jl, y] = shift_x(shift_z(block, -o[2]), -o[0])
-
     def inside(y):
         return 0 <= y < Y
 
-    for k in range(NB):
-        for y in range(Y):
-            if inside(y - bonds[k][1]):
-                mirror(k, y)
-
-    def place(sx, sz):
-        n = (sx + 1) * 3 + sz + 1
-        return n - (n > 4)
-
-    def spread_field(m, slot):
-        for o in range(O):
-            rows = slice(o * Cw, (o + 1) * Cw)
-            base = V[m, slot, rows, :]
-            for sz in (-1, 0, 1):
-                turned = shift_z(base, sz)
-                for sx in (-1, 0, 1):
-                    if (sx, sz) != (0, 0):
-                        VS[place(sx, sz), slot, rows, :] = shift_x(turned, sx)
+    def mirror(within):
+        groups = {}
+        for k, o in enumerate(bonds):
+            for y in range(Y):
+                if inside(y - o[1]) == within:
+                    groups.setdefault((-o[0], -o[2]), []).extend((k, jl, y) for jl in range(p.JT))
+        for (sx, sz), members in groups.items():
+            blocks = [M[jl, y + 1 - bonds[k][1], k * ROWS:(k + 1) * ROWS, :] for k, jl, y in members]
+            if (sx, sz) != (0, 0):
+                at = place(sx, sz) * L
+                moved = jnp.dot(halves(jnp.concatenate(blocks, axis=0)), PM[:, at:at + L], preferred_element_type=f32)
+                blocks = [moved[n * ROWS:(n + 1) * ROWS] for n in range(len(members))]
+            for (k, jl, y), block in zip(members, blocks):
+                MB[k, jl, y] = block
+
+    mirror(True)
+
+    def spread_field(m, slots):
+        rows = len(slots) * OC
+        for n, slot in enumerate(slots):
+            LH[n * OC:(n + 1) * OC, :] = halves(V[m, slot])
+        for n in range(0, 8, 2):
+            at = slice(n * L, (n + 2) * L)
+            moved = jnp.dot(LH[0:rows, :], PM[:, at], preferred_element_type=f32)
+            for q, slot in enumerate(slots):
+                VS[slot, :, at] = moved[q * OC:(q + 1) * OC]
 
     def add_bonds(acc, m, y, steps):
         for k, o in enumerate(bonds):
@@ -278,7 +294,8 @@
                 sx, sz = sign * o[0], sign * o[2]
                 for j in range(O):
                     rows = slice(j * Cw, (j + 1) * Cw)
-                    v = V[m, slot, rows, :] if (sx, sz) == (0, 0) else VS[place(sx, sz), slot, rows, :]
+                    at = place(sx, sz) * L
+                    v = V[m, slot, rows, :] if (sx, sz) == (0, 0) else VS[slot, rows, at:at + L]
                     for i in range(O):
                         if sign > 0:
                             row = k * ROWS + i * HALFJ + j // p.JT
@@ -339,8 +356,7 @@
 
     theta = None
     for m in range(ITERS):
-        for slot in range(1, Y + 1):
-            spread_field(m, slot)
+        spread_field(m, range(1, Y + 1))
         for y in range(Y):
             acc = zeros()
             add_bonds(acc, m, y, [s for s in (-1, 0, 1) if inside(y + s)])
@@ -355,12 +371,9 @@
         arrived(halo)
         if m == 0:
             arrived(coef_halo)
-            for k in range(NB):
-                for y in range(Y):
-                    if not inside(y - bonds[k][1]):
-                        mirror(k, y)
-        for slot, y, s in ((0, 0, -1), (Y + 1, Y - 1, 1)):
-            spread_field(m, slot)
+            mirror(False)
+        spread_field(m, (0, Y + 1))
+        for y, s in ((0, -1), (Y - 1, 1)):
             acc = take(m + 1, y)
             add_bonds(acc, m, y, [s])
             add_onsite(acc, m, y, theta)
@@ -480,7 +493,7 @@
     onsite = onsite_blocks.reshape(O * O * X * Y, Z)
     levels = orbital_levels.reshape(O * X * Y, Z)
     dma = pltpu.SemaphoreType.DMA
-    vmem, anywhere = pl.BlockSpec(memory_space=pltpu.VMEM), pl.BlockSpec(memory_space=pl.ANY)
+    anywhere = pl.BlockSpec(memory_space=pl.ANY)
 
     def scratch(*shape):
         return pltpu.VMEM(shape, f32)
@@ -488,11 +501,17 @@
     outs = pl.pallas_call(
         functools.partial(kernel, p),
         out_shape=(jax.ShapeDtypeStruct(right.shape, f32),) * 2,
-        in_specs=[anywhere, anywhere] + [vmem] * 4,
+        in_specs=[anywhere] * 6,
         out_specs=(anywhere, anywhere),
         scratch_shapes=[
             scratch(X * Y * Z * H * O, LANES),
             scratch(O * O * X * Y * Z, NB),
+            pltpu.VMEM(opened.shape, jnp.int32),
+            scratch(*onsite.shape),
+            scratch(*levels.shape),
+            scratch(1, cols),
+            pltpu.VMEM((2 * L, 8 * L), jnp.bfloat16),
+            pltpu.VMEM((Y * p.OC, 2 * L), jnp.bfloat16),
             scratch(cols, p.HL),
             scratch(S, p.Cw, p.HL),
             scratch(p.CR, LANES),
@@ -500,7 +519,7 @@
             scratch(p.JT, Y + 2, p.CR, L),
             scratch(NB, p.JT, Y, ROWS, L),
             scratch(ITERS + 1, Y + 2, p.OC, L),
-            scratch(8, Y + 2, p.OC, L),
+            scratch(Y + 2, p.OC, 8 * L),
             scratch(ITERS, S, p.Cw, p.HL),
             scratch(ITERS, cols, p.HL),
             scratch(p.ny, ROWS, LANES),

time: 52.2 us -> 45.1 us (0.86)
  Pallas kernels: 48.9 us -> 41.8 us
    pallas_call x1, Pallas kernels: 48.9 us -> 41.8 us  [per_device(): pl.pallas_call(functools.partial(kernel, p), out_shape=(jax.ShapeDtypeStr...]
where the time goes in v2:
time: 45.1 us; the launch traced here: 44.9 us
  Pallas kernels  41.8 us (93%)
  local copies, waits for them, and re-layouts  2.42 us (5%)
  between operations  0.65 us (1%)
    pallas_call x1, Pallas kernels, per_device(): pl.pallas_call(functools.partial(kernel, p), out_shape=(jax.ShapeDtypeStr...  41.8 us
    unnamed x4, local copies, waits for them, and re-layouts  2.42 us

profile of v2, /device:TPU:0, one launch (start us, length us, event | category | flops | bytes accessed | tf_op | source)
XLA Modules:
  0.0 44.9 jit_solution(2543178985512966333)
XLA Ops:
  0.6 41.8 %shard_map.77 = (f32[4,4,32,128]{3,2,1,0:T(8,128)}, f32[4,4,32,128]{3,2,1,0:T(8,128)}) custom-call(f32[4,4,32,128]{3,2,1,0:T(8,128)} %bitcast.25, f32[1024,13]{1,0:T(8,128)} %bitcast.24, s32[64,13]{1,0:T(8,128)} %bitcast.29, f32[256,4]{1,0:T(8,128)} %bitcast.28, f32[64,4]{1,0:T(8,128)} %bitcast.30, f32[1,256]{1,0:T(1,128)} %bitcast.31), custom_call_target="tpu_custom_call" | custom-call | tf_op jit(solution)/shard_map/pallas_call | solution.py:501
  42.5 0.0 copy-start
  42.5 1.7 %copy.13 = f32[4,4,4,4,256]{4,3,2,1,0:T(4,128)} copy(f32[4,4,4,4,256]{4,3,2,1,0:T(4,128)} %bitcast.27) | data formatting | bytes 524288
  44.2 0.0 copy-done
  44.2 0.7 %copy.14 = f32[4,4,4,4,256]{4,3,2,1,0:T(4,128)} copy(f32[4,4,4,4,256]{4,3,2,1,0:T(4,128)S(1)} %bitcast.26) | data formatting | bytes 524288
Async XLA Ops:
  42.5 1.7 %copy-start = (f32[4,4,32,128]{3,2,1,0:T(8,128)S(1)}, f32[4,4,32,128]{3,2,1,0:T(8,128)}, u32[]{:S(2)}) copy-start(f32[4,4,32,128]{3,2,1,0:T(8,128)} %get-tuple-element.5) | copy-start | bytes 786436

commit v3 on v2

--- a/solution.py
+++ b/solution.py
@@ -44,8 +44,8 @@
 
 
 def kernel(plan, rs_hbm, bb_hbm, open_hbm, onsite_hbm, level_hbm, shift_hbm, sol_hbm, res_hbm,
-           RS, BB, open_ref, onsite_ref, level_ref, shift_ref, PM, LH, T, RB, CS, CR, M, MB, V, VS, SB, YB, MG, TG, WQ, OS,
-           in_sem, a_s, a_r, c_s, c_r, hv_s, hv_r, hm_s, hm_r, th_s, th_r, y_s, y_r, mo_s, mo_r, w_s, w_r):
+           RS, BB, open_ref, onsite_ref, level_ref, shift_ref, PM, LH, T, RB, CS, CR, M, MB, V, VS, SB, YB, EM, SR, TG, OS,
+           in_sem, a_s, a_r, c_s, c_r, hv_s, hv_r, hm_s, hm_r, th_s, th_r, y_s, y_r, e_s, e_r):
     p = plan
     X, Y, Z, O, S, L, l, G, Cw, H, OC = p.X, p.Y, p.Z, p.O, p.S, p.L, p.l, p.G, p.Cw, p.H, p.OC
     f32 = jnp.float32
@@ -335,6 +335,27 @@
 
     moments = []
     home_copies = []
+
+    everyone = [(g, r) for g in range(p.ny) for r in range(S) if (g, r) != (0, 0)]
+
+    def tell(part, values):
+        table = jnp.zeros((Cw, LANES), f32)
+        for n, value in enumerate(values):
+            table = jnp.where(lane128 == n, value, table)
+        if Cw < LANES:
+            table = jnp.concatenate([table, jnp.zeros((LANES - Cw, LANES), f32)], axis=0)
+        table = jnp.transpose(table)
+        line = table[0:1]
+        for n in range(1, len(values)):
+            line = line + roll(table[n:n + 1], n * Cw)
+        EM[part, ay, me] = line
+        SR[part] = line
+        copies = []
+        for n, (g, r) in enumerate(everyone):
+            d = lax.rem(me + r, S)
+            device = (lax.div(d, p.nz), lax.rem(ay + g, p.ny), lax.rem(d, p.nz))
+            copies.append(send(SR.at[part], EM.at[part, ay, me], e_s.at[part, n], e_r.at[part, n], device))
+        return copies
 
     def go_home(m):
         for t in range(p.HT):
@@ -388,23 +409,27 @@
         moments.append(moment(m, m + 1))
         if m + 1 < ITERS:
             moments.append(moment(m + 1, m + 1))
-
-    table = jnp.zeros((Cw, LANES), f32)
-    for n, value in enumerate(moments):
-        table = jnp.where(lane128 == n, value, table)
-    if Cw < LANES:
-        table = jnp.concatenate([table, jnp.zeros((LANES - Cw, LANES), f32)], axis=0)
-    MG[ay] = jnp.transpose(table)[0:ROWS, :]
-    arrived([send(MG.at[ay], MG.at[ay], mo_s.at[r - 1], mo_r.at[r - 1], along(r)) for r in range(1, p.ny)])
-    total = MG[0]
-    for n in range(1, p.ny):
-        total = total + MG[n]
-    m_of = [total[n:n + 1, :] for n in range(2 * ITERS)]
-    shift = jnp.zeros((1, LANES), f32)
-    for d in range(S):
-        h, at = divmod(d * Cw, LANES)
-        shift = jnp.where(me == d, roll(shift_ref[:, h * LANES:(h + 1) * LANES], -at), shift)
-    shift = shift + theta
+        if m + 2 == ITERS:
+            early = len(moments) - 1
+            told = tell(0, moments[:early])
+    told = told + tell(1, moments[early:])
+
+    shift = jnp.concatenate([
+        roll(shift_ref[:, d * Cw // LANES * LANES:(d * Cw // LANES + 1) * LANES], -(d * Cw % LANES)) for d in range(S)
+    ], axis=0) + theta
+    arrived(told)
+
+    def total(part):
+        rows = []
+        for d in range(S):
+            line = EM[part, 0, d]
+            for n in range(1, p.ny):
+                line = line + EM[part, n, d]
+            rows.append(line)
+        return jnp.concatenate(rows, axis=0)
+
+    sums = [total(0), total(1)]
+    m_of = [roll(sums[n >= early], -(n - early * (n >= early)) * Cw) for n in range(2 * ITERS)]
 
     def inner(u, v):
         out = None
@@ -425,7 +450,7 @@
                 out.append(u[a])
         return out
 
-    one = jnp.ones((1, LANES), f32)
+    one = jnp.ones((S, LANES), f32)
     answer, residual, direction, norm = [], [one], [one], m_of[0]
     for turn in range(ITERS):
         image = [shift * direction[0]]
@@ -440,35 +465,30 @@
             direction = plus(residual, direction, fresh / norm)
             norm = fresh
     factors = answer + residual
-    WQ[me] = jnp.concatenate(factors + [jnp.zeros((ROWS - len(factors), LANES), f32)], axis=0)
-    factor_copies = []
-    for r in range(1, S):
-        d, device = mate(r)
-        factor_copies.append(send(WQ.at[me], WQ.at[me], w_s.at[r - 1], w_r.at[r - 1], device))
-    arrived(factor_copies)
+    lines = jnp.concatenate(factors, axis=0)
+    spare = -lines.shape[0] % LANES
+    if spare:
+        lines = jnp.concatenate([lines, jnp.zeros((spare, LANES), f32)], axis=0)
+    column = jnp.transpose(lines)
     arrived(home_copies)
 
     outs = []
-    for h in range(H):
-        lines = jnp.zeros((ROWS, LANES), f32)
-        per = LANES // Cw
-        for n in range(per):
-            d = h * per + n
-            lines = jnp.where(lane128 // Cw == n, roll(WQ[d], n * Cw), lines)
-        column = jnp.transpose(lines)
-        rows = slice(h * LANES, (h + 1) * LANES)
-        basis = [T[rows, :]] + [YB[n, rows, :] for n in range(ITERS)]
-        for which, hbm in ((0, sol_hbm), (1, res_hbm)):
-            at = which * ITERS
-            field = column[:, at:at + 1] * basis[0]
-            for n in range(1, ITERS + which):
-                field = field + column[:, at + n:at + n + 1] * basis[n]
-            field = jnp.transpose(field)
+    for which, hbm in ((0, sol_hbm), (1, res_hbm)):
+        for h in range(H):
+            fields = []
+            for d in range(h * LANES // Cw, (h + 1) * LANES // Cw):
+                rows = slice(d * Cw, (d + 1) * Cw)
+                field = None
+                for n in range(ITERS + which):
+                    at = (which * ITERS + n) * S + d
+                    term = column[0:Cw, at:at + 1] * (T[rows, :] if n == 0 else YB[n - 1, rows, :])
+                    field = term if field is None else field + term
+                fields.append(field)
+            field = jnp.transpose(jnp.concatenate(fields, axis=0))
             for y in range(Y):
                 for o in range(O):
                     n = (y * O + o) * l
                     OS[which, pl.ds(y * X * Z * step + h * O + o, l, stride=step), :] = field[n:n + l, :]
-    for which, hbm in ((0, sol_hbm), (1, res_hbm)):
         for x in range(X):
             for y in range(Y):
                 n = Z * H * O
@@ -522,16 +542,16 @@
             scratch(Y + 2, p.OC, 8 * L),
             scratch(ITERS, S, p.Cw, p.HL),
             scratch(ITERS, cols, p.HL),
+            scratch(2, p.ny, S, 1, LANES),
+            scratch(2, 1, LANES),
             scratch(p.ny, ROWS, LANES),
-            scratch(p.ny, ROWS, LANES),
-            scratch(S, ROWS, LANES),
             scratch(2, X * Y * Z * H * O, LANES),
             dma((2 * X * Y,)),
             dma((S - 1,)), dma((S - 1,)), dma((S - 1,)), dma((S - 1,)),
             dma((ITERS, 2)), dma((ITERS, 2)), dma((3,)), dma((3,)),
             dma((p.ny - 1,)), dma((p.ny - 1,)),
             dma((ITERS, S - 1)), dma((ITERS, S - 1)),
-            dma((p.ny - 1,)), dma((p.ny - 1,)), dma((S - 1,)), dma((S - 1,)),
+            dma((2, p.ny * S - 1)), dma((2, p.ny * S - 1)),
         ],
         compiler_params=pltpu.CompilerParams(
             collective_id=0, has_side_effects=True, vmem_limit_bytes=60 * 1024 * 1024

time: 45.1 us -> 43.7 us (0.969)
  Pallas kernels: 41.8 us -> 40.4 us
    pallas_call x1, Pallas kernels: 41.8 us -> 40.4 us  [per_device(): pl.pallas_call(functools.partial(kernel, p), out_shape=(jax.ShapeDtypeStr...]
where the time goes in v3:
time: 43.7 us; the launch traced here: 43.4 us
  Pallas kernels  40.4 us (92%)
  local copies, waits for them, and re-layouts  2.42 us (6%)
  between operations  0.65 us (1%)
    pallas_call x1, Pallas kernels, per_device(): pl.pallas_call(functools.partial(kernel, p), out_shape=(jax.ShapeDtypeStr...  40.4 us
    unnamed x4, local copies, waits for them, and re-layouts  2.42 us

profile of v3, /device:TPU:0, one launch (start us, length us, event | category | flops | bytes accessed | tf_op | source)
XLA Modules:
  0.0 43.4 jit_solution(16345511260219807127)
XLA Ops:
  0.6 40.4 %shard_map.77 = (f32[4,4,32,128]{3,2,1,0:T(8,128)}, f32[4,4,32,128]{3,2,1,0:T(8,128)}) custom-call(f32[4,4,32,128]{3,2,1,0:T(8,128)} %bitcast.25, f32[1024,13]{1,0:T(8,128)} %bitcast.24, s32[64,13]{1,0:T(8,128)} %bitcast.29, f32[256,4]{1,0:T(8,128)} %bitcast.28, f32[64,4]{1,0:T(8,128)} %bitcast.30, f32[1,256]{1,0:T(1,128)} %bitcast.31), custom_call_target="tpu_custom_call" | custom-call | tf_op jit(solution)/shard_map/pallas_call | solution.py:521
  41.0 0.0 copy-start
  41.0 1.7 %copy.13 = f32[4,4,4,4,256]{4,3,2,1,0:T(4,128)} copy(f32[4,4,4,4,256]{4,3,2,1,0:T(4,128)} %bitcast.27) | data formatting | bytes 524288
  42.7 0.0 copy-done
  42.7 0.7 %copy.14 = f32[4,4,4,4,256]{4,3,2,1,0:T(4,128)} copy(f32[4,4,4,4,256]{4,3,2,1,0:T(4,128)S(1)} %bitcast.26) | data formatting | bytes 524288
Async XLA Ops:
  41.0 1.7 %copy-start = (f32[4,4,32,128]{3,2,1,0:T(8,128)S(1)}, f32[4,4,32,128]{3,2,1,0:T(8,128)}, u32[]{:S(2)}) copy-start(f32[4,4,32,128]{3,2,1,0:T(8,128)} %get-tuple-element.5) | copy-start | bytes 786436

commit v4 on v3

--- a/solution.py
+++ b/solution.py
@@ -43,8 +43,8 @@
         assert self.tiles == ROWS and self.S % self.G == 0 and self.Cw % ROWS == 0
 
 
-def kernel(plan, rs_hbm, bb_hbm, open_hbm, onsite_hbm, level_hbm, shift_hbm, sol_hbm, res_hbm,
-           RS, BB, open_ref, onsite_ref, level_ref, shift_ref, PM, LH, T, RB, CS, CR, M, MB, V, VS, SB, YB, EM, SR, TG, OS,
+def kernel(plan, rs_hbm, bb_hbm, open_hbm, onsite_hbm, level_hbm, shift_hbm, T, YB, FX,
+           RS, BB, open_ref, onsite_ref, level_ref, shift_ref, PM, LH, RB, CS, CR, M, MB, V, VS, SB, EM, SR, TG,
            in_sem, a_s, a_r, c_s, c_r, hv_s, hv_r, hm_s, hm_r, th_s, th_r, y_s, y_r, e_s, e_r):
     p = plan
     X, Y, Z, O, S, L, l, G, Cw, H, OC = p.X, p.Y, p.Z, p.O, p.S, p.L, p.l, p.G, p.Cw, p.H, p.OC
@@ -469,9 +469,17 @@
     spare = -lines.shape[0] % LANES
     if spare:
         lines = jnp.concatenate([lines, jnp.zeros((spare, LANES), f32)], axis=0)
-    column = jnp.transpose(lines)
+    for at in range(0, lines.shape[0], LANES):
+        FX[:, at:at + LANES] = jnp.transpose(lines[at:at + LANES])
     arrived(home_copies)
-
+    for copy in pending:
+        copy.wait_send()
+
+
+def combine(plan, T, YB, FX, sol_hbm, res_hbm, OS, sem):
+    p = plan
+    X, Y, Z, O, S, l, Cw, H = p.X, p.Y, p.Z, p.O, p.S, p.l, p.Cw, p.H
+    step = H * O
     outs = []
     for which, hbm in ((0, sol_hbm), (1, res_hbm)):
         for h in range(H):
@@ -481,7 +489,7 @@
                 field = None
                 for n in range(ITERS + which):
                     at = (which * ITERS + n) * S + d
-                    term = column[0:Cw, at:at + 1] * (T[rows, :] if n == 0 else YB[n - 1, rows, :])
+                    term = FX[0:Cw, at:at + 1] * (T[rows, :] if n == 0 else YB[n - 1, rows, :])
                     field = term if field is None else field + term
                 fields.append(field)
             field = jnp.transpose(jnp.concatenate(fields, axis=0))
@@ -493,13 +501,11 @@
             for y in range(Y):
                 n = Z * H * O
                 copy = pltpu.make_async_copy(
-                    OS.at[which, pl.ds((y * X + x) * n, n)], hbm.at[x, y], in_sem.at[(which * X + x) * Y + y])
+                    OS.at[which, pl.ds((y * X + x) * n, n)], hbm.at[x, y], sem.at[(which * X + x) * Y + y])
                 copy.start()
                 outs.append(copy)
     for copy in outs:
         copy.wait()
-    for copy in pending:
-        copy.wait_send()
 
 
 def per_device(peers, right_side, bond_blocks, bond_open, onsite_blocks, orbital_levels, column_shift):
@@ -513,16 +519,18 @@
     onsite = onsite_blocks.reshape(O * O * X * Y, Z)
     levels = orbital_levels.reshape(O * X * Y, Z)
     dma = pltpu.SemaphoreType.DMA
-    anywhere = pl.BlockSpec(memory_space=pl.ANY)
+    vmem, anywhere = pl.BlockSpec(memory_space=pltpu.VMEM), pl.BlockSpec(memory_space=pl.ANY)
 
     def scratch(*shape):
         return pltpu.VMEM(shape, f32)
 
-    outs = pl.pallas_call(
+    flat = (p.cols, p.HL)
+    width = -(-(2 * ITERS + 1) * S // LANES) * LANES
+    made = pl.pallas_call(
         functools.partial(kernel, p),
-        out_shape=(jax.ShapeDtypeStruct(right.shape, f32),) * 2,
-        in_specs=[anywhere] * 6,
-        out_specs=(anywhere, anywhere),
+        out_shape=(scratch(*flat), scratch(ITERS, *flat), scratch(LANES, width)),
+        in_specs=[pl.BlockSpec(memory_space=pltpu.HBM)] * 6,
+        out_specs=(vmem,) * 3,
         scratch_shapes=[
             scratch(X * Y * Z * H * O, LANES),
             scratch(O * O * X * Y * Z, NB),
@@ -532,7 +540,6 @@
             scratch(1, cols),
             pltpu.VMEM((2 * L, 8 * L), jnp.bfloat16),
             pltpu.VMEM((Y * p.OC, 2 * L), jnp.bfloat16),
-            scratch(cols, p.HL),
             scratch(S, p.Cw, p.HL),
             scratch(p.CR, LANES),
             scratch(S, p.CR, LANES),
@@ -541,12 +548,10 @@
             scratch(ITERS + 1, Y + 2, p.OC, L),
             scratch(Y + 2, p.OC, 8 * L),
             scratch(ITERS, S, p.Cw, p.HL),
-            scratch(ITERS, cols, p.HL),
             scratch(2, p.ny, S, 1, LANES),
             scratch(2, 1, LANES),
             scratch(p.ny, ROWS, LANES),
-            scratch(2, X * Y * Z * H * O, LANES),
-            dma((2 * X * Y,)),
+            dma((X * Y + 5,)),
             dma((S - 1,)), dma((S - 1,)), dma((S - 1,)), dma((S - 1,)),
             dma((ITERS, 2)), dma((ITERS, 2)), dma((3,)), dma((3,)),
             dma((p.ny - 1,)), dma((p.ny - 1,)),
@@ -554,9 +559,18 @@
             dma((2, p.ny * S - 1)), dma((2, p.ny * S - 1)),
         ],
         compiler_params=pltpu.CompilerParams(
-            collective_id=0, has_side_effects=True, vmem_limit_bytes=60 * 1024 * 1024
+            collective_id=0, has_side_effects=True, vmem_limit_bytes=40 * 1024 * 1024
         ),
-    )(right, blocks, opened, onsite, levels, column_shift[None])
+    )(*(pltpu.with_memory_space_constraint(v, pltpu.HBM)
+        for v in (right, blocks, opened, onsite, levels, column_shift[None])))
+    outs = pl.pallas_call(
+        functools.partial(combine, p),
+        out_shape=(jax.ShapeDtypeStruct(right.shape, f32),) * 2,
+        in_specs=[vmem] * 3,
+        out_specs=(anywhere, anywhere),
+        scratch_shapes=[scratch(2, X * Y * Z * H * O, LANES), dma((2 * X * Y,))],
+        compiler_params=pltpu.CompilerParams(vmem_limit_bytes=16 * 1024 * 1024),
+    )(*made)
 
     def back(v):
         return v.reshape(X, Y, Z, H, O, LANES).transpose(0, 1, 2, 4, 3, 5).reshape(right_side.shape)

time: 43.7 us -> 41.4 us (0.947)
  local copies, waits for them, and re-layouts: 2.42 us -> 0 us
    unnamed x4 -> x0, local copies, waits for them, and re-layouts: 2.42 us -> none
    pallas_call x1 -> x2, Pallas kernels: 40.4 us -> 40.6 us  [the longest x1 39 us: per_device(): pl.pallas_call(functools.partial(kernel, p), out_shape=(scratch(*flat), s...]
where the time goes in v4:
time: 41.4 us; the launch traced here: 41.2 us
  Pallas kernels  40.6 us (98%)
  between operations  0.64 us (2%)
    pallas_call x1, Pallas kernels, per_device(): pl.pallas_call(functools.partial(kernel, p), out_shape=(scratch(*flat), s...  39 us
    pallas_call x1, Pallas kernels, per_device(): pl.pallas_call(functools.partial(combine, p), out_shape=(jax.ShapeDtypeSt...  1.53 us

profile of v4, /device:TPU:0, one launch (start us, length us, event | category | flops | bytes accessed | tf_op | source)
XLA Modules:
  0.0 41.2 jit_solution(13364402117599811012)
XLA Ops:
  0.6 39.0 %shard_map.77 = (f32[256,256]{1,0:T(8,128)S(1)}, f32[3,256,256]{2,1,0:T(8,128)S(1)}, f32[128,128]{1,0:T(8,128)S(1)}) custom-call(f32[4,4,32,128]{3,2,1,0:T(8,128)} %bitcast.25, f32[1024,13]{1,0:T(8,128)} %bitcast.24, s32[64,13]{1,0:T(8,128)} %bitcast.27, f32[256,4]{1,0:T(8,128)} %bitcast.26, f32[64,4]{1,0:T(8,128)} %bitcast.28, f32[1,256]{1,0:T(1,128)} %bitcast.29), custom_call_target="tpu_custom_call" | custom-call | tf_op jit(solution)/shard_map/pallas_call | solution.py:529
  39.7 1.5 %shard_map.78 = (f32[4,4,32,128]{3,2,1,0:T(8,128)}, f32[4,4,32,128]{3,2,1,0:T(8,128)}) custom-call(f32[256,256]{1,0:T(8,128)S(1)} %get-tuple-element.7.T, f32[3,256,256]{2,1,0:T(8,128)S(1)} %get-tuple-element.8.YB, f32[128,128]{1,0:T(8,128)S(1)} %get-tuple-element.9.FX), custom_call_target="tpu_custom_call" | custom-call | tf_op jit(solution)/shard_map/pallas_call | solution.py:566

commit v5 on v4

--- a/solution.py
+++ b/solution.py
@@ -40,12 +40,15 @@
         self.tiles = orb * orb // self.JT
         self.CR = (NB + 1) * self.tiles
         self.OC = orb * self.Cw
+        edge = sum(n for _, n in ahead_runs + behind_runs)
+        self.HR = (-(-edge // (LANES // (self.JT * self.l))) + 1) * ROWS
+        assert self.H * orb == ROWS
         assert self.tiles == ROWS and self.S % self.G == 0 and self.Cw % ROWS == 0
 
 
-def kernel(plan, rs_hbm, bb_hbm, open_hbm, onsite_hbm, level_hbm, shift_hbm, T, YB, FX,
-           RS, BB, open_ref, onsite_ref, level_ref, shift_ref, PM, LH, RB, CS, CR, M, MB, V, VS, SB, EM, SR, TG,
-           in_sem, a_s, a_r, c_s, c_r, hv_s, hv_r, hm_s, hm_r, th_s, th_r, y_s, y_r, e_s, e_r):
+def kernel(plan, rs_hbm, bb_hbm, open_hbm, onsite_hbm, level_hbm, shift_hbm, BT, FX,
+           RS, BB, open_ref, onsite_ref, level_ref, shift_ref, PM, LH, T, YB, ZC, HS, HC, RB, CS, CR, M, MB, V, VS, SB, EM, SR, TG,
+           in_sem, a_s, a_r, c_s, c_r, hv_s, hv_r, hm_s, hm_r, ho_s, ho_r, th_s, th_r, y_s, y_r, e_s, e_r):
     p = plan
     X, Y, Z, O, S, L, l, G, Cw, H, OC = p.X, p.Y, p.Z, p.O, p.S, p.L, p.l, p.G, p.Cw, p.H, p.OC
     f32 = jnp.float32
@@ -148,6 +151,7 @@
             RS[pl.ds(y * X * Z * step + h * O + o, l, stride=step), :] for y in range(Y) for o in range(O)
         ], axis=0)
         T[h * LANES:(h + 1) * LANES, :] = jnp.transpose(rows)
+    BT[0] = RS[...]
     make_shifts()
     pl.semaphore_wait(barrier, S - 1 + p.ny - 1)
     field_copies = []
@@ -176,6 +180,7 @@
     pair = [jnp.sum(onsite[n * XY:(n + 1) * XY], axis=0, keepdims=True) for n in range(O * O)]
     diagonal = [jnp.sum(level[n * XY:(n + 1) * XY], axis=0, keepdims=True) for n in range(O)]
     j_low = lane128 // (Y * l)
+    diagonal_sum = jnp.zeros((1, LANES), f32)
     for i in range(O):
         for jh in range(O // p.JT):
             line = jnp.zeros((1, LANES), f32)
@@ -184,10 +189,12 @@
                 term = 0.5 * (pair[i * O + j] + pair[j * O + i])
                 if i == j:
                     term = term + diagonal[i]
+                    diagonal_sum = diagonal_sum + jnp.where(j_low == 0, term, 0.0)
                 line = jnp.where(j_low == jl, term, line)
             row = NB * ROWS + i * (O // p.JT) + jh
             CS[row:row + 1, :] = line
 
+    diagonal_sum = jnp.sum(diagonal_sum, axis=1, keepdims=True)
     for copy in small_loads[2:]:
         copy.wait()
     is_open = open_ref[...].astype(f32)
@@ -205,6 +212,13 @@
             if gap:
                 out = jnp.where(source_lane - lane128 == gap, roll(block, -gap), out)
         CS[pl.ds(t, NB, stride=ROWS), :] = out[0:NB, :]
+    early_halo = []
+    for n, (run, way) in enumerate([(run, 1) for run in ahead_runs] + [(run, -1) for run in behind_runs]):
+        early_halo.append(send(
+            CS.at[pl.ds(run[0] * ROWS, run[1] * ROWS)], ZC.at[n], hm_s.at[n], hm_r.at[n], along(way)))
+    TG[ay] = jnp.broadcast_to(diagonal_sum, (ROWS, LANES))
+    early_halo += [
+        send(TG.at[ay], TG.at[ay], th_s.at[r - 1], th_r.at[r - 1], along(r)) for r in range(1, p.ny)]
     coef_copies = []
     for r in range(1, S):
         d, device = mate(r)
@@ -220,6 +234,16 @@
     def arrived(copies):
         for copy in copies:
             copy.wait_recv()
+
+    def spread_field(m, slots):
+        rows = len(slots) * OC
+        for n, slot in enumerate(slots):
+            LH[n * OC:(n + 1) * OC, :] = halves(V[m, slot])
+        for n in range(0, 8, 2):
+            at = slice(n * L, (n + 2) * L)
+            moved = jnp.dot(LH[0:rows, :], PM[:, at], preferred_element_type=f32)
+            for q, slot in enumerate(slots):
+                VS[slot, :, at] = moved[q * OC:(q + 1) * OC]
 
     arrived(field_copies)
     for t in range(p.HT):
@@ -231,6 +255,46 @@
                 V[0, y + 1, o * Cw:(o + 1) * Cw, at:at + LANES] = blocks[n]
     halo = halo_field(0)
 
+    arrived(early_halo)
+    outer = [(n, q, run[0] + q, slot, y) for n, (run, slot, y) in enumerate(
+        [(run, 0, Y - 1) for run in ahead_runs] + [(run, Y + 1, 0) for run in behind_runs]) for q in range(run[1])]
+    unit = p.JT * l
+    U = LANES // unit
+    for v in range(0, len(outer), U):
+        packed = jnp.zeros((ROWS, LANES), f32)
+        for q, (n, at, k, slot, y) in enumerate(outer[v:v + U]):
+            block = ZC[n, at * ROWS:(at + 1) * ROWS, :]
+            for jl in range(p.JT):
+                to = q * unit + jl * l
+                packed = jnp.where(block_of == to // l, roll(block, to - jl * Y * l - y * l), packed)
+        HS[v // U * ROWS:(v // U + 1) * ROWS, :] = packed
+    part = TG[0]
+    for n in range(1, p.ny):
+        part = part + TG[n]
+    HS[p.HR - ROWS:p.HR, :] = part
+    outer_copies = []
+    for r in range(1, S):
+        d, device = mate(r)
+        outer_copies.append(send(HS, HC.at[me], ho_s.at[r - 1], ho_r.at[r - 1], device))
+    HC[me] = HS[...]
+    spread_field(0, range(1, Y + 1))
+
+    def take_outer():
+        arrived(outer_copies)
+        for first in range(0, S, G):
+            blocks = butterfly([HC[first + n, 0:p.HR - ROWS, :] for n in range(G)])
+            at = first // G * LANES
+            for n, (_, _, k, slot, y) in enumerate(outer):
+                v, q = divmod(n, U)
+                for jl in range(p.JT):
+                    M[jl, slot, k * ROWS:(k + 1) * ROWS, at:at + LANES] = (
+                        blocks[q * p.JT + jl][v * ROWS:(v + 1) * ROWS])
+        mirror(False)
+        total = HC[0, p.HR - ROWS:p.HR - ROWS + 1, 0:1]
+        for n in range(1, S):
+            total = total + HC[n, p.HR - ROWS:p.HR - ROWS + 1, 0:1]
+        return total * (1.0 / (p.ny * Y * L * O))
+
     arrived(coef_copies)
     for first in range(0, S, G):
         blocks = butterfly([CR[first + n] for n in range(G)])
@@ -238,22 +302,7 @@
         for n in range(G):
             jl, y = divmod(n, Y)
             M[jl, y + 1, :, at:at + LANES] = blocks[n]
-    coef_halo = []
-    for n, (run, y_from, y_to_slot, way) in enumerate(
-            [(run, Y, 0, 1) for run in ahead_runs] + [(run, 1, Y + 1, -1) for run in behind_runs]):
-        rows = pl.ds(run[0] * ROWS, run[1] * ROWS)
-        coef_halo.append(send(
-            M.at[:, y_from, rows], M.at[:, y_to_slot, rows], hm_s.at[n], hm_r.at[n], along(way)))
-
     HALFJ = O // p.JT
-    diag_rows = [(i % p.JT, NB * ROWS + i * HALFJ + i // p.JT) for i in range(O)]
-    part = jnp.zeros((1, L), f32)
-    for y in range(1, Y + 1):
-        for jl, row in diag_rows:
-            part = part + M[jl, y, row:row + 1, :]
-    TG[ay] = jnp.broadcast_to(jnp.sum(part, axis=1, keepdims=True), (ROWS, LANES))
-    theta_copies = [
-        send(TG.at[ay], TG.at[ay], th_s.at[r - 1], th_r.at[r - 1], along(r)) for r in range(1, p.ny)]
 
     def inside(y):
         return 0 <= y < Y
@@ -274,16 +323,6 @@
                 MB[k, jl, y] = block
 
     mirror(True)
-
-    def spread_field(m, slots):
-        rows = len(slots) * OC
-        for n, slot in enumerate(slots):
-            LH[n * OC:(n + 1) * OC, :] = halves(V[m, slot])
-        for n in range(0, 8, 2):
-            at = slice(n * L, (n + 2) * L)
-            moved = jnp.dot(LH[0:rows, :], PM[:, at], preferred_element_type=f32)
-            for q, slot in enumerate(slots):
-                VS[slot, :, at] = moved[q * OC:(q + 1) * OC]
 
     def add_bonds(acc, m, y, steps):
         for k, o in enumerate(bonds):
@@ -339,15 +378,12 @@
     everyone = [(g, r) for g in range(p.ny) for r in range(S) if (g, r) != (0, 0)]
 
     def tell(part, values):
+        sublane = lax.broadcasted_iota(jnp.int32, (Cw, LANES), 0)
+        spot = lax.broadcasted_iota(jnp.int32, (Cw, LANES), 1)
         table = jnp.zeros((Cw, LANES), f32)
         for n, value in enumerate(values):
-            table = jnp.where(lane128 == n, value, table)
-        if Cw < LANES:
-            table = jnp.concatenate([table, jnp.zeros((LANES - Cw, LANES), f32)], axis=0)
-        table = jnp.transpose(table)
-        line = table[0:1]
-        for n in range(1, len(values)):
-            line = line + roll(table[n:n + 1], n * Cw)
+            table = jnp.where(spot == sublane + n * Cw, value, table)
+        line = jnp.sum(table, axis=0, keepdims=True)
         EM[part, ay, me] = line
         SR[part] = line
         copies = []
@@ -377,22 +413,16 @@
 
     theta = None
     for m in range(ITERS):
-        spread_field(m, range(1, Y + 1))
+        if m > 0:
+            spread_field(m, range(1, Y + 1))
         for y in range(Y):
             acc = zeros()
             add_bonds(acc, m, y, [s for s in (-1, 0, 1) if inside(y + s)])
             put(acc, m + 1, y)
         if m == 0:
             moments.append(moment(0, 0))
-            arrived(theta_copies)
-            theta = TG[0][0:1, 0:1]
-            for n in range(1, p.ny):
-                theta = theta + TG[n][0:1, 0:1]
-            theta = theta * (1.0 / (p.ny * Y * L * O))
+            theta = take_outer()
         arrived(halo)
-        if m == 0:
-            arrived(coef_halo)
-            mirror(False)
         spread_field(m, (0, Y + 1))
         for y, s in ((0, -1), (Y - 1, 1)):
             acc = take(m + 1, y)
@@ -405,7 +435,8 @@
             acc = take(m + 1, y)
             add_onsite(acc, m, y, theta)
             put(acc, m + 1, y)
-        go_home(m + 1)
+        if m + 1 < ITERS:
+            go_home(m + 1)
         moments.append(moment(m, m + 1))
         if m + 1 < ITERS:
             moments.append(moment(m + 1, m + 1))
@@ -413,10 +444,23 @@
             early = len(moments) - 1
             told = tell(0, moments[:early])
     told = told + tell(1, moments[early:])
+    go_home(ITERS)
 
     shift = jnp.concatenate([
         roll(shift_ref[:, d * Cw // LANES * LANES:(d * Cw // LANES + 1) * LANES], -(d * Cw % LANES)) for d in range(S)
     ], axis=0) + theta
+
+    def turn_home(n):
+        arrived(home_copies[n * (S - 1):(n + 1) * (S - 1)])
+        for h in range(H):
+            field = jnp.transpose(YB[n, h * LANES:(h + 1) * LANES, :])
+            for y in range(Y):
+                for o in range(O):
+                    at = (y * O + o) * l
+                    BT[n + 1, pl.ds(y * X * Z * step + h * O + o, l, stride=step), :] = field[at:at + l, :]
+
+    for n in range(ITERS):
+        turn_home(n)
     arrived(told)
 
     def total(part):
@@ -465,41 +509,38 @@
             direction = plus(residual, direction, fresh / norm)
             norm = fresh
     factors = answer + residual
-    lines = jnp.concatenate(factors, axis=0)
-    spare = -lines.shape[0] % LANES
-    if spare:
-        lines = jnp.concatenate([lines, jnp.zeros((spare, LANES), f32)], axis=0)
-    for at in range(0, lines.shape[0], LANES):
-        FX[:, at:at + LANES] = jnp.transpose(lines[at:at + LANES])
-    arrived(home_copies)
+    per = LANES // Cw
+    half = lax.broadcasted_iota(jnp.int32, (H * O, LANES), 0) // O
+    for n, factor in enumerate(factors):
+        turned = [roll(factor, q * Cw) for q in range(per)]
+        block = jnp.zeros((H * O, LANES), f32)
+        for h in range(H):
+            line = turned[0][h * per:h * per + 1]
+            for q in range(1, per):
+                line = jnp.where(lane128 // Cw == q, turned[q][h * per + q:h * per + q + 1], line)
+            block = jnp.where(half == h, line, block)
+        FX[n] = block
     for copy in pending:
         copy.wait_send()
 
 
-def combine(plan, T, YB, FX, sol_hbm, res_hbm, OS, sem):
+def combine(plan, BT, FX, sol_hbm, res_hbm, OS, sem):
     p = plan
-    X, Y, Z, O, S, l, Cw, H = p.X, p.Y, p.Z, p.O, p.S, p.l, p.Cw, p.H
-    step = H * O
+    X, Y, n = p.X, p.Y, p.Z * p.H * p.O
+    group = p.H * p.O
     outs = []
     for which, hbm in ((0, sol_hbm), (1, res_hbm)):
-        for h in range(H):
-            fields = []
-            for d in range(h * LANES // Cw, (h + 1) * LANES // Cw):
-                rows = slice(d * Cw, (d + 1) * Cw)
-                field = None
-                for n in range(ITERS + which):
-                    at = (which * ITERS + n) * S + d
-                    term = FX[0:Cw, at:at + 1] * (T[rows, :] if n == 0 else YB[n - 1, rows, :])
-                    field = term if field is None else field + term
-                fields.append(field)
-            field = jnp.transpose(jnp.concatenate(fields, axis=0))
-            for y in range(Y):
-                for o in range(O):
-                    n = (y * O + o) * l
-                    OS[which, pl.ds(y * X * Z * step + h * O + o, l, stride=step), :] = field[n:n + l, :]
+        for y in range(Y):
+            for x in range(X):
+                base = (y * X + x) * n
+                for at in range(base, base + n, group):
+                    rows = slice(at, at + group)
+                    field = FX[which * ITERS] * BT[0, rows, :]
+                    for q in range(1, ITERS + which):
+                        field = field + FX[which * ITERS + q] * BT[q, rows, :]
+                    OS[which, rows, :] = field
         for x in range(X):
             for y in range(Y):
-                n = Z * H * O
                 copy = pltpu.make_async_copy(
                     OS.at[which, pl.ds((y * X + x) * n, n)], hbm.at[x, y], sem.at[(which * X + x) * Y + y])
                 copy.start()
@@ -525,12 +566,11 @@
         return pltpu.VMEM(shape, f32)
 
     flat = (p.cols, p.HL)
-    width = -(-(2 * ITERS + 1) * S // LANES) * LANES
     made = pl.pallas_call(
         functools.partial(kernel, p),
-        out_shape=(scratch(*flat), scratch(ITERS, *flat), scratch(LANES, width)),
+        out_shape=(scratch(ITERS + 1, X * Y * Z * H * O, LANES), scratch(2 * ITERS + 1, H * O, LANES)),
         in_specs=[pl.BlockSpec(memory_space=pltpu.HBM)] * 6,
-        out_specs=(vmem,) * 3,
+        out_specs=(vmem,) * 2,
         scratch_shapes=[
             scratch(X * Y * Z * H * O, LANES),
             scratch(O * O * X * Y * Z, NB),
@@ -540,6 +580,11 @@
             scratch(1, cols),
             pltpu.VMEM((2 * L, 8 * L), jnp.bfloat16),
             pltpu.VMEM((Y * p.OC, 2 * L), jnp.bfloat16),
+            scratch(*flat),
+            scratch(ITERS, *flat),
+            scratch(3, 3 * ROWS, LANES),
+            scratch(p.HR, LANES),
+            scratch(S, p.HR, LANES),
             scratch(S, p.Cw, p.HL),
             scratch(p.CR, LANES),
             scratch(S, p.CR, LANES),
@@ -554,6 +599,7 @@
             dma((X * Y + 5,)),
             dma((S - 1,)), dma((S - 1,)), dma((S - 1,)), dma((S - 1,)),
             dma((ITERS, 2)), dma((ITERS, 2)), dma((3,)), dma((3,)),
+            dma((S - 1,)), dma((S - 1,)),
             dma((p.ny - 1,)), dma((p.ny - 1,)),
             dma((ITERS, S - 1)), dma((ITERS, S - 1)),
             dma((2, p.ny * S - 1)), dma((2, p.ny * S - 1)),
@@ -566,7 +612,7 @@
     outs = pl.pallas_call(
         functools.partial(combine, p),
         out_shape=(jax.ShapeDtypeStruct(right.shape, f32),) * 2,
-        in_specs=[vmem] * 3,
+        in_specs=[vmem] * 2,
         out_specs=(anywhere, anywhere),
         scratch_shapes=[scratch(2, X * Y * Z * H * O, LANES), dma((2 * X * Y,))],
         compiler_params=pltpu.CompilerParams(vmem_limit_bytes=16 * 1024 * 1024),

time: 41.4 us -> 39.8 us (0.961)
  Pallas kernels: 40.6 us -> 38.9 us
    pallas_call x1, Pallas kernels: 39 us -> 37.8 us  [per_device(): pl.pallas_call(functools.partial(kernel, p), out_shape=(scratch(ITERS + 1...]
    pallas_call x1, Pallas kernels: 1.53 us -> 1.1 us  [per_device(): pl.pallas_call(functools.partial(combine, p), out_shape=(jax.ShapeDtypeSt...]
where the time goes in v5:
time: 39.8 us; the launch traced here: 39.6 us
  Pallas kernels  38.9 us (98%)
  between operations  0.64 us (2%)
    pallas_call x1, Pallas kernels, per_device(): pl.pallas_call(functools.partial(kernel, p), out_shape=(scratch(ITERS + 1...  37.8 us
    pallas_call x1, Pallas kernels, per_device(): pl.pallas_call(functools.partial(combine, p), out_shape=(jax.ShapeDtypeSt...  1.1 us

profile of v5, /device:TPU:0, one launch (start us, length us, event | category | flops | bytes accessed | tf_op | source)
XLA Modules:
  0.0 39.6 jit_solution(9035329750968354276)
XLA Ops:
  0.6 37.8 %shard_map.77 = (f32[4,512,128]{2,1,0:T(8,128)S(1)}, f32[7,8,128]{2,1,0:T(8,128)S(1)}) custom-call(f32[4,4,32,128]{3,2,1,0:T(8,128)} %bitcast.25, f32[1024,13]{1,0:T(8,128)} %bitcast.24, s32[64,13]{1,0:T(8,128)} %bitcast.27, f32[256,4]{1,0:T(8,128)} %bitcast.26, f32[64,4]{1,0:T(8,128)} %bitcast.28, f32[1,256]{1,0:T(1,128)} %bitcast.29), custom_call_target="tpu_custom_call" | custom-call | tf_op jit(solution)/shard_map/pallas_call | solution.py:569
  38.5 1.1 %shard_map.78 = (f32[4,4,32,128]{3,2,1,0:T(8,128)}, f32[4,4,32,128]{3,2,1,0:T(8,128)}) custom-call(f32[4,512,128]{2,1,0:T(8,128)S(1)} %get-tuple-element.6.BT, f32[7,8,128]{2,1,0:T(8,128)S(1)} %get-tuple-element.7.FX), custom_call_target="tpu_custom_call" | custom-call | tf_op jit(solution)/shard_map/pallas_call | solution.py:612

commit v6 on v5

--- a/solution.py
+++ b/solution.py
@@ -146,9 +146,14 @@
     for copy in loads:
         copy.wait()
     step = H * O
+    order = list(range(1, Y - 1)) + [0, Y - 1]
+
+    def group(n):
+        return order[n // O], n % O
+
     for h in range(H):
         rows = jnp.concatenate([
-            RS[pl.ds(y * X * Z * step + h * O + o, l, stride=step), :] for y in range(Y) for o in range(O)
+            RS[pl.ds(y * X * Z * step + h * O + o, l, stride=step), :] for y in order for o in range(O)
         ], axis=0)
         T[h * LANES:(h + 1) * LANES, :] = jnp.transpose(rows)
     BT[0] = RS[...]
@@ -219,10 +224,13 @@
     TG[ay] = jnp.broadcast_to(diagonal_sum, (ROWS, LANES))
     early_halo += [
         send(TG.at[ay], TG.at[ay], th_s.at[r - 1], th_r.at[r - 1], along(r)) for r in range(1, p.ny)]
+    partner = (ax + 1 - 2 * lax.rem(ax, 2), ay, az)
+    even = [(dx, dz) for dz in range(p.nz) for dx in range(0, p.nx, 2) if (dx, dz) != (0, 0)]
     coef_copies = []
-    for r in range(1, S):
-        d, device = mate(r)
-        coef_copies.append(send(CS, CR.at[me], c_s.at[r - 1], c_r.at[r - 1], device))
+    for n, (dx, dz) in enumerate(even):
+        device = (lax.rem(ax + dx, p.nx), ay, lax.rem(az + dz, p.nz))
+        coef_copies.append(send(CS, CR.at[me], c_s.at[n], c_r.at[n], device))
+    relays = [send(CS, CR.at[me], c_s.at[len(even)], c_r.at[len(even)], partner)]
     CR[me] = CS[...]
 
     def halo_field(m):
@@ -251,7 +259,7 @@
             blocks = butterfly([RB[first + n, :, t * LANES:(t + 1) * LANES] for n in range(G)])
             at = first // G * LANES
             for n in range(G):
-                y, o = divmod(t * G + n, O)
+                y, o = group(t * G + n)
                 V[0, y + 1, o * Cw:(o + 1) * Cw, at:at + LANES] = blocks[n]
     halo = halo_field(0)
 
@@ -295,7 +303,12 @@
             total = total + HC[n, p.HR - ROWS:p.HR - ROWS + 1, 0:1]
         return total * (1.0 / (p.ny * Y * L * O))
 
-    arrived(coef_copies)
+    for n, (dx, dz) in enumerate(even):
+        coef_copies[n].wait_recv()
+        s = lax.rem(ax + (p.nx - dx), p.nx) * p.nz + lax.rem(az + (p.nz - dz), p.nz)
+        at = len(even) + 1 + n
+        relays.append(send(CR.at[s], CR.at[s], c_s.at[at], c_r.at[at], partner))
+    arrived(relays)
     for first in range(0, S, G):
         blocks = butterfly([CR[first + n] for n in range(G)])
         at = first // G * LANES
@@ -373,7 +386,7 @@
         return jnp.sum(total, axis=1, keepdims=True)
 
     moments = []
-    home_copies = []
+    home_copies = {}
 
     everyone = [(g, r) for g in range(p.ny) for r in range(S) if (g, r) != (0, 0)]
 
@@ -393,27 +406,29 @@
             copies.append(send(SR.at[part], EM.at[part, ay, me], e_s.at[part, n], e_r.at[part, n], device))
         return copies
 
-    def go_home(m):
-        for t in range(p.HT):
-            for first in range(0, S, G):
-                at = first // G * LANES
-                blocks = []
-                for n in range(G):
-                    y, o = divmod(t * G + n, O)
-                    blocks.append(V[m, y + 1, o * Cw:(o + 1) * Cw, at:at + LANES])
-                blocks = butterfly(blocks)
-                for n in range(G):
-                    SB[m - 1, first + n, :, t * LANES:(t + 1) * LANES] = blocks[n]
+    def go_home(m, t):
+        for first in range(0, S, G):
+            at = first // G * LANES
+            blocks = []
+            for n in range(G):
+                y, o = group(t * G + n)
+                blocks.append(V[m, y + 1, o * Cw:(o + 1) * Cw, at:at + LANES])
+            blocks = butterfly(blocks)
+            for n in range(G):
+                SB[m - 1, t, first + n] = blocks[n]
         mine = pl.ds(pl.multiple_of(me * Cw, ROWS), Cw)
+        copies = home_copies.setdefault(m, [])
         for r in range(1, S):
             d, device = mate(r)
-            home_copies.append(send(
-                SB.at[m - 1, d], YB.at[m - 1, mine], y_s.at[m - 1, r - 1], y_r.at[m - 1, r - 1], device))
-        YB[m - 1, mine] = SB[m - 1, me]
+            copies.append(send(SB.at[m - 1, t, d], YB.at[m - 1, t, mine],
+                               y_s.at[m - 1, t, r - 1], y_r.at[m - 1, t, r - 1], device))
+        YB[m - 1, t, mine] = SB[m - 1, t, me]
 
     theta = None
     for m in range(ITERS):
         if m > 0:
+            M[0, 0, 0:ROWS, :] = jnp.zeros((ROWS, L), f32)
+            MB[NB, 0, 0] = jnp.zeros((ROWS, L), f32)
             spread_field(m, range(1, Y + 1))
         for y in range(Y):
             acc = zeros()
@@ -422,6 +437,12 @@
         if m == 0:
             moments.append(moment(0, 0))
             theta = take_outer()
+        for y in range(1, Y - 1):
+            acc = take(m + 1, y)
+            add_onsite(acc, m, y, theta)
+            put(acc, m + 1, y)
+        if m + 1 == ITERS:
+            go_home(ITERS, 0)
         arrived(halo)
         spread_field(m, (0, Y + 1))
         for y, s in ((0, -1), (Y - 1, 1)):
@@ -431,12 +452,8 @@
             put(acc, m + 1, y)
         if m + 1 < ITERS:
             halo = halo_field(m + 1)
-        for y in range(1, Y - 1):
-            acc = take(m + 1, y)
-            add_onsite(acc, m, y, theta)
-            put(acc, m + 1, y)
-        if m + 1 < ITERS:
-            go_home(m + 1)
+        for t in range(1 if m + 1 == ITERS else 0, p.HT if m + 1 < ITERS else 1):
+            go_home(m + 1, t)
         moments.append(moment(m, m + 1))
         if m + 1 < ITERS:
             moments.append(moment(m + 1, m + 1))
@@ -444,20 +461,21 @@
             early = len(moments) - 1
             told = tell(0, moments[:early])
     told = told + tell(1, moments[early:])
-    go_home(ITERS)
+    for t in range(1, p.HT):
+        go_home(ITERS, t)
 
     shift = jnp.concatenate([
         roll(shift_ref[:, d * Cw // LANES * LANES:(d * Cw // LANES + 1) * LANES], -(d * Cw % LANES)) for d in range(S)
     ], axis=0) + theta
 
     def turn_home(n):
-        arrived(home_copies[n * (S - 1):(n + 1) * (S - 1)])
+        arrived(home_copies[n + 1])
         for h in range(H):
-            field = jnp.transpose(YB[n, h * LANES:(h + 1) * LANES, :])
-            for y in range(Y):
-                for o in range(O):
-                    at = (y * O + o) * l
-                    BT[n + 1, pl.ds(y * X * Z * step + h * O + o, l, stride=step), :] = field[at:at + l, :]
+            for t in range(p.HT):
+                field = jnp.transpose(YB[n, t, h * LANES:(h + 1) * LANES, :])
+                for q in range(G):
+                    y, o = group(t * G + q)
+                    BT[n + 1, pl.ds(y * X * Z * step + h * O + o, l, stride=step), :] = field[q * l:(q + 1) * l, :]
 
     for n in range(ITERS):
         turn_home(n)
@@ -581,7 +599,7 @@
             pltpu.VMEM((2 * L, 8 * L), jnp.bfloat16),
             pltpu.VMEM((Y * p.OC, 2 * L), jnp.bfloat16),
             scratch(*flat),
-            scratch(ITERS, *flat),
+            scratch(ITERS, p.HT, cols, LANES),
             scratch(3, 3 * ROWS, LANES),
             scratch(p.HR, LANES),
             scratch(S, p.HR, LANES),
@@ -589,10 +607,10 @@
             scratch(p.CR, LANES),
             scratch(S, p.CR, LANES),
             scratch(p.JT, Y + 2, p.CR, L),
-            scratch(NB, p.JT, Y, ROWS, L),
+            scratch(NB + 1, p.JT, Y, ROWS, L),
             scratch(ITERS + 1, Y + 2, p.OC, L),
             scratch(Y + 2, p.OC, 8 * L),
-            scratch(ITERS, S, p.Cw, p.HL),
+            scratch(ITERS, p.HT, S, p.Cw, LANES),
             scratch(2, p.ny, S, 1, LANES),
             scratch(2, 1, LANES),
             scratch(p.ny, ROWS, LANES),
@@ -601,7 +619,7 @@
             dma((ITERS, 2)), dma((ITERS, 2)), dma((3,)), dma((3,)),
             dma((S - 1,)), dma((S - 1,)),
             dma((p.ny - 1,)), dma((p.ny - 1,)),
-            dma((ITERS, S - 1)), dma((ITERS, S - 1)),
+            dma((ITERS, p.HT, S - 1)), dma((ITERS, p.HT, S - 1)),
             dma((2, p.ny * S - 1)), dma((2, p.ny * S - 1)),
         ],
         compiler_params=pltpu.CompilerParams(

time: 39.8 us -> 38.9 us (0.977)
  Pallas kernels: 38.9 us -> 38.1 us
    pallas_call x1, Pallas kernels: 37.8 us -> 37 us  [per_device(): pl.pallas_call(functools.partial(kernel, p), out_shape=(scratch(ITERS + 1...]
where the time goes in v6:
time: 38.9 us; the launch traced here: 38.7 us
  Pallas kernels  38.1 us (98%)
  between operations  0.64 us (2%)
    pallas_call x1, Pallas kernels, per_device(): pl.pallas_call(functools.partial(kernel, p), out_shape=(scratch(ITERS + 1...  37 us
    pallas_call x1, Pallas kernels, per_device(): pl.pallas_call(functools.partial(combine, p), out_shape=(jax.ShapeDtypeSt...  1.1 us

profile of v6, /device:TPU:0, one launch (start us, length us, event | category | flops | bytes accessed | tf_op | source)
XLA Modules:
  0.0 38.7 jit_solution(17749543403424663957)
XLA Ops:
  0.6 37.0 %shard_map.77 = (f32[4,512,128]{2,1,0:T(8,128)S(1)}, f32[7,8,128]{2,1,0:T(8,128)S(1)}) custom-call(f32[4,4,32,128]{3,2,1,0:T(8,128)} %bitcast.25, f32[1024,13]{1,0:T(8,128)} %bitcast.24, s32[64,13]{1,0:T(8,128)} %bitcast.27, f32[256,4]{1,0:T(8,128)} %bitcast.26, f32[64,4]{1,0:T(8,128)} %bitcast.28, f32[1,256]{1,0:T(1,128)} %bitcast.29), custom_call_target="tpu_custom_call" | custom-call | tf_op jit(solution)/shard_map/pallas_call | solution.py:587
  37.6 1.1 %shard_map.78 = (f32[4,4,32,128]{3,2,1,0:T(8,128)}, f32[4,4,32,128]{3,2,1,0:T(8,128)}) custom-call(f32[4,512,128]{2,1,0:T(8,128)S(1)} %get-tuple-element.6.BT, f32[7,8,128]{2,1,0:T(8,128)S(1)} %get-tuple-element.7.FX), custom_call_target="tpu_custom_call" | custom-call | tf_op jit(solution)/shard_map/pallas_call | solution.py:630

commit v7 on v6

--- a/solution.py
+++ b/solution.py
@@ -39,7 +39,9 @@
         self.JT = LANES // (self.Y * self.l)
         self.tiles = orb * orb // self.JT
         self.CR = (NB + 1) * self.tiles
-        self.OC = orb * self.Cw
+        self.NG = 2 if self.Cw % (2 * ROWS) == 0 else 1
+        self.Cg = self.Cw // self.NG
+        self.OC = orb * self.Cg
         edge = sum(n for _, n in ahead_runs + behind_runs)
         self.HR = (-(-edge // (LANES // (self.JT * self.l))) + 1) * ROWS
         assert self.H * orb == ROWS
@@ -51,6 +53,7 @@
            in_sem, a_s, a_r, c_s, c_r, hv_s, hv_r, hm_s, hm_r, ho_s, ho_r, th_s, th_r, y_s, y_r, e_s, e_r):
     p = plan
     X, Y, Z, O, S, L, l, G, Cw, H, OC = p.X, p.Y, p.Z, p.O, p.S, p.L, p.l, p.G, p.Cw, p.H, p.OC
+    NG, Cg = p.NG, p.Cg
     f32 = jnp.float32
     ax, ay, az = (lax.axis_index(name) for name in AXES)
     me = ax * p.nz + az
@@ -233,25 +236,25 @@
     relays = [send(CS, CR.at[me], c_s.at[len(even)], c_r.at[len(even)], partner)]
     CR[me] = CS[...]
 
-    def halo_field(m):
+    def halo_field(m, g):
         return [
-            send(V.at[m, 1], V.at[m, Y + 1], hv_s.at[m, 0], hv_r.at[m, 0], along(-1)),
-            send(V.at[m, Y], V.at[m, 0], hv_s.at[m, 1], hv_r.at[m, 1], along(1)),
+            send(V.at[m, 1, g], V.at[m, Y + 1, g], hv_s.at[m, g, 0], hv_r.at[m, g, 0], along(-1)),
+            send(V.at[m, Y, g], V.at[m, 0, g], hv_s.at[m, g, 1], hv_r.at[m, g, 1], along(1)),
         ]
 
     def arrived(copies):
         for copy in copies:
             copy.wait_recv()
 
-    def spread_field(m, slots):
+    def spread_field(m, slots, g):
         rows = len(slots) * OC
         for n, slot in enumerate(slots):
-            LH[n * OC:(n + 1) * OC, :] = halves(V[m, slot])
+            LH[g, n * OC:(n + 1) * OC, :] = halves(V[m, slot, g])
         for n in range(0, 8, 2):
             at = slice(n * L, (n + 2) * L)
-            moved = jnp.dot(LH[0:rows, :], PM[:, at], preferred_element_type=f32)
+            moved = jnp.dot(LH[g, 0:rows, :], PM[:, at], preferred_element_type=f32)
             for q, slot in enumerate(slots):
-                VS[slot, :, at] = moved[q * OC:(q + 1) * OC]
+                VS[slot, g, :, at] = moved[q * OC:(q + 1) * OC]
 
     arrived(field_copies)
     for t in range(p.HT):
@@ -260,8 +263,9 @@
             at = first // G * LANES
             for n in range(G):
                 y, o = group(t * G + n)
-                V[0, y + 1, o * Cw:(o + 1) * Cw, at:at + LANES] = blocks[n]
-    halo = halo_field(0)
+                for g in range(NG):
+                    V[0, y + 1, g, o * Cg:(o + 1) * Cg, at:at + LANES] = blocks[n][g * Cg:(g + 1) * Cg]
+    halo = [halo_field(0, g) for g in range(NG)]
 
     arrived(early_halo)
     outer = [(n, q, run[0] + q, slot, y) for n, (run, slot, y) in enumerate(
@@ -285,7 +289,8 @@
         d, device = mate(r)
         outer_copies.append(send(HS, HC.at[me], ho_s.at[r - 1], ho_r.at[r - 1], device))
     HC[me] = HS[...]
-    spread_field(0, range(1, Y + 1))
+    for g in range(NG):
+        spread_field(0, range(1, Y + 1), g)
 
     def take_outer():
         arrived(outer_copies)
@@ -337,7 +342,9 @@
 
     mirror(True)
 
-    def add_bonds(acc, m, y, steps):
+    zero = [0, lax.div(ax, p.nx), lax.div(ay, p.ny)]
+
+    def add_bonds(acc, m, y, steps, g):
         for k, o in enumerate(bonds):
             for sign in (1, -1):
                 if sign * o[1] not in steps:
@@ -345,45 +352,48 @@
                 slot = y + 1 + sign * o[1]
                 sx, sz = sign * o[0], sign * o[2]
                 for j in range(O):
-                    rows = slice(j * Cw, (j + 1) * Cw)
+                    rows = slice(j * Cg, (j + 1) * Cg)
                     at = place(sx, sz) * L
-                    v = V[m, slot, rows, :] if (sx, sz) == (0, 0) else VS[slot, rows, at:at + L]
+                    v = V[m, slot, g, rows, :] if (sx, sz) == (0, 0) else VS[slot, g, rows, at:at + L]
                     for i in range(O):
                         if sign > 0:
                             row = k * ROWS + i * HALFJ + j // p.JT
-                            c = M[j % p.JT, y + 1, row:row + 1, :]
+                            c = M[zero[m] + j % p.JT, y + 1, row:row + 1, :]
                         else:
                             row = j * HALFJ + i // p.JT
-                            c = MB[k, i % p.JT, y, row:row + 1, :]
+                            c = MB[zero[m] + k, i % p.JT, y, row:row + 1, :]
                         acc[i] = acc[i] + c * v
 
-    def add_onsite(acc, m, y, theta):
+    def add_onsite(acc, m, y, theta, g):
         for j in range(O):
-            v = V[m, y + 1, j * Cw:(j + 1) * Cw, :]
+            v = V[m, y + 1, g, j * Cg:(j + 1) * Cg, :]
             for i in range(O):
                 row = NB * ROWS + i * HALFJ + j // p.JT
-                c = M[j % p.JT, y + 1, row:row + 1, :]
+                c = M[zero[m] + j % p.JT, y + 1, row:row + 1, :]
                 if i == j:
                     c = c - theta
                 acc[i] = acc[i] + c * v
 
-    def put(acc, m, y):
+    def put(acc, m, y, g):
         for i in range(O):
-            V[m, y + 1, i * Cw:(i + 1) * Cw, :] = acc[i]
-
-    def take(m, y):
-        return [V[m, y + 1, i * Cw:(i + 1) * Cw, :] for i in range(O)]
+            V[m, y + 1, g, i * Cg:(i + 1) * Cg, :] = acc[i]
+
+    def take(m, y, g):
+        return [V[m, y + 1, g, i * Cg:(i + 1) * Cg, :] for i in range(O)]
 
     def zeros():
-        return [jnp.zeros((Cw, L), f32) for _ in range(O)]
+        return [jnp.zeros((Cg, L), f32) for _ in range(O)]
 
     def moment(a, b):
-        total = jnp.zeros((Cw, L), f32)
-        for y in range(Y):
-            for i in range(O):
-                rows = slice(i * Cw, (i + 1) * Cw)
-                total = total + V[a, y + 1, rows, :] * V[b, y + 1, rows, :]
-        return jnp.sum(total, axis=1, keepdims=True)
+        sums = []
+        for g in range(NG):
+            total = jnp.zeros((Cg, L), f32)
+            for y in range(Y):
+                for i in range(O):
+                    rows = slice(i * Cg, (i + 1) * Cg)
+                    total = total + V[a, y + 1, g, rows, :] * V[b, y + 1, g, rows, :]
+            sums.append(jnp.sum(total, axis=1, keepdims=True))
+        return jnp.concatenate(sums, axis=0)
 
     moments = []
     home_copies = {}
@@ -406,63 +416,69 @@
             copies.append(send(SR.at[part], EM.at[part, ay, me], e_s.at[part, n], e_r.at[part, n], device))
         return copies
 
-    def go_home(m, t):
-        for first in range(0, S, G):
-            at = first // G * LANES
-            blocks = []
-            for n in range(G):
-                y, o = group(t * G + n)
-                blocks.append(V[m, y + 1, o * Cw:(o + 1) * Cw, at:at + LANES])
-            blocks = butterfly(blocks)
-            for n in range(G):
-                SB[m - 1, t, first + n] = blocks[n]
+    def go_home(m, tiles):
+        for t in tiles:
+            for first in range(0, S, G):
+                at = first // G * LANES
+                blocks = []
+                for n in range(G):
+                    y, o = group(t * G + n)
+                    blocks.append(jnp.concatenate(
+                        [V[m, y + 1, g, o * Cg:(o + 1) * Cg, at:at + LANES] for g in range(NG)], axis=0))
+                blocks = butterfly(blocks)
+                for n in range(G):
+                    SB[m - 1, t, first + n] = blocks[n]
         mine = pl.ds(pl.multiple_of(me * Cw, ROWS), Cw)
         copies = home_copies.setdefault(m, [])
+        at, n = tiles[0], len(tiles)
         for r in range(1, S):
             d, device = mate(r)
-            copies.append(send(SB.at[m - 1, t, d], YB.at[m - 1, t, mine],
-                               y_s.at[m - 1, t, r - 1], y_r.at[m - 1, t, r - 1], device))
-        YB[m - 1, t, mine] = SB[m - 1, t, me]
+            copies.append(send(SB.at[m - 1, pl.ds(at, n), d], YB.at[m - 1, pl.ds(at, n), mine],
+                               y_s.at[m - 1, at, r - 1], y_r.at[m - 1, at, r - 1], device))
+        for t in tiles:
+            YB[m - 1, t, mine] = SB[m - 1, t, me]
 
     theta = None
     for m in range(ITERS):
-        if m > 0:
-            M[0, 0, 0:ROWS, :] = jnp.zeros((ROWS, L), f32)
-            MB[NB, 0, 0] = jnp.zeros((ROWS, L), f32)
-            spread_field(m, range(1, Y + 1))
-        for y in range(Y):
-            acc = zeros()
-            add_bonds(acc, m, y, [s for s in (-1, 0, 1) if inside(y + s)])
-            put(acc, m + 1, y)
+        last = m + 1 == ITERS
+        for g in range(NG):
+            if m > 0:
+                spread_field(m, range(1, Y + 1), g)
+            for y in range(Y):
+                acc = zeros()
+                if m > 0 and 0 < y < Y - 1:
+                    add_onsite(acc, m, y, theta, g)
+                add_bonds(acc, m, y, [s for s in (-1, 0, 1) if inside(y + s)], g)
+                put(acc, m + 1, y, g)
         if m == 0:
             moments.append(moment(0, 0))
             theta = take_outer()
-        for y in range(1, Y - 1):
-            acc = take(m + 1, y)
-            add_onsite(acc, m, y, theta)
-            put(acc, m + 1, y)
-        if m + 1 == ITERS:
-            go_home(ITERS, 0)
-        arrived(halo)
-        spread_field(m, (0, Y + 1))
-        for y, s in ((0, -1), (Y - 1, 1)):
-            acc = take(m + 1, y)
-            add_bonds(acc, m, y, [s])
-            add_onsite(acc, m, y, theta)
-            put(acc, m + 1, y)
-        if m + 1 < ITERS:
-            halo = halo_field(m + 1)
-        for t in range(1 if m + 1 == ITERS else 0, p.HT if m + 1 < ITERS else 1):
-            go_home(m + 1, t)
-        moments.append(moment(m, m + 1))
-        if m + 1 < ITERS:
-            moments.append(moment(m + 1, m + 1))
-        if m + 2 == ITERS:
+            for g in range(NG):
+                for y in range(1, Y - 1):
+                    acc = take(m + 1, y, g)
+                    add_onsite(acc, m, y, theta, g)
+                    put(acc, m + 1, y, g)
+        if last:
+            go_home(ITERS, [0])
             early = len(moments) - 1
             told = tell(0, moments[:early])
+        for g in range(NG):
+            arrived(halo[g])
+            spread_field(m, (0, Y + 1), g)
+            for y, s in ((0, -1), (Y - 1, 1)):
+                acc = take(m + 1, y, g)
+                add_bonds(acc, m, y, [s], g)
+                add_onsite(acc, m, y, theta, g)
+                put(acc, m + 1, y, g)
+            if not last:
+                halo[g] = halo_field(m + 1, g)
+        if not last:
+            go_home(m + 1, list(range(p.HT)))
+        moments.append(moment(m, m + 1))
+        if not last:
+            moments.append(moment(m + 1, m + 1))
     told = told + tell(1, moments[early:])
-    for t in range(1, p.HT):
-        go_home(ITERS, t)
+    go_home(ITERS, list(range(1, p.HT)))
 
     shift = jnp.concatenate([
         roll(shift_ref[:, d * Cw // LANES * LANES:(d * Cw // LANES + 1) * LANES], -(d * Cw % LANES)) for d in range(S)
@@ -597,7 +613,7 @@
             scratch(*levels.shape),
             scratch(1, cols),
             pltpu.VMEM((2 * L, 8 * L), jnp.bfloat16),
-            pltpu.VMEM((Y * p.OC, 2 * L), jnp.bfloat16),
+            pltpu.VMEM((p.NG, Y * p.OC, 2 * L), jnp.bfloat16),
             scratch(*flat),
             scratch(ITERS, p.HT, cols, LANES),
             scratch(3, 3 * ROWS, LANES),
@@ -607,16 +623,16 @@
             scratch(p.CR, LANES),
             scratch(S, p.CR, LANES),
             scratch(p.JT, Y + 2, p.CR, L),
-            scratch(NB + 1, p.JT, Y, ROWS, L),
-            scratch(ITERS + 1, Y + 2, p.OC, L),
-            scratch(Y + 2, p.OC, 8 * L),
+            scratch(NB, p.JT, Y, ROWS, L),
+            scratch(ITERS + 1, Y + 2, p.NG, p.OC, L),
+            scratch(Y + 2, p.NG, p.OC, 8 * L),
             scratch(ITERS, p.HT, S, p.Cw, LANES),
             scratch(2, p.ny, S, 1, LANES),
             scratch(2, 1, LANES),
             scratch(p.ny, ROWS, LANES),
             dma((X * Y + 5,)),
             dma((S - 1,)), dma((S - 1,)), dma((S - 1,)), dma((S - 1,)),
-            dma((ITERS, 2)), dma((ITERS, 2)), dma((3,)), dma((3,)),
+            dma((ITERS, p.NG, 2)), dma((ITERS, p.NG, 2)), dma((3,)), dma((3,)),
             dma((S - 1,)), dma((S - 1,)),
             dma((p.ny - 1,)), dma((p.ny - 1,)),
             dma((ITERS, p.HT, S - 1)), dma((ITERS, p.HT, S - 1)),

time: 38.9 us -> 37.6 us (0.967)
  Pallas kernels: 38.1 us -> 36.8 us
    pallas_call x1, Pallas kernels: 37 us -> 35.7 us  [per_device(): pl.pallas_call(functools.partial(kernel, p), out_shape=(scratch(ITERS + 1...]
where the time goes in v7:
time: 37.6 us; the launch traced here: 37.4 us
  Pallas kernels  36.8 us (98%)
  between operations  0.64 us (2%)
    pallas_call x1, Pallas kernels, per_device(): pl.pallas_call(functools.partial(kernel, p), out_shape=(scratch(ITERS + 1...  35.7 us
    pallas_call x1, Pallas kernels, per_device(): pl.pallas_call(functools.partial(combine, p), out_shape=(jax.ShapeDtypeSt...  1.1 us

profile of v7, /device:TPU:0, one launch (start us, length us, event | category | flops | bytes accessed | tf_op | source)
XLA Modules:
  0.0 37.4 jit_solution(7380886893665086266)
XLA Ops:
  0.6 35.7 %shard_map.77 = (f32[4,512,128]{2,1,0:T(8,128)S(1)}, f32[7,8,128]{2,1,0:T(8,128)S(1)}) custom-call(f32[4,4,32,128]{3,2,1,0:T(8,128)} %bitcast.25, f32[1024,13]{1,0:T(8,128)} %bitcast.24, s32[64,13]{1,0:T(8,128)} %bitcast.27, f32[256,4]{1,0:T(8,128)} %bitcast.26, f32[64,4]{1,0:T(8,128)} %bitcast.28, f32[1,256]{1,0:T(1,128)} %bitcast.29), custom_call_target="tpu_custom_call" | custom-call | tf_op jit(solution)/shard_map/pallas_call | solution.py:603
  36.3 1.1 %shard_map.78 = (f32[4,4,32,128]{3,2,1,0:T(8,128)}, f32[4,4,32,128]{3,2,1,0:T(8,128)}) custom-call(f32[4,512,128]{2,1,0:T(8,128)S(1)} %get-tuple-element.6.BT, f32[7,8,128]{2,1,0:T(8,128)S(1)} %get-tuple-element.7.FX), custom_call_target="tpu_custom_call" | custom-call | tf_op jit(solution)/shard_map/pallas_call | solution.py:646

commit v8 on v7

--- a/solution.py
+++ b/solution.py
@@ -342,8 +342,6 @@
 
     mirror(True)
 
-    zero = [0, lax.div(ax, p.nx), lax.div(ay, p.ny)]
-
     def add_bonds(acc, m, y, steps, g):
         for k, o in enumerate(bonds):
             for sign in (1, -1):
@@ -358,10 +356,10 @@
                     for i in range(O):
                         if sign > 0:
                             row = k * ROWS + i * HALFJ + j // p.JT
-                            c = M[zero[m] + j % p.JT, y + 1, row:row + 1, :]
+                            c = M[j % p.JT, y + 1, row:row + 1, :]
                         else:
                             row = j * HALFJ + i // p.JT
-                            c = MB[zero[m] + k, i % p.JT, y, row:row + 1, :]
+                            c = MB[k, i % p.JT, y, row:row + 1, :]
                         acc[i] = acc[i] + c * v
 
     def add_onsite(acc, m, y, theta, g):
@@ -369,7 +367,7 @@
             v = V[m, y + 1, g, j * Cg:(j + 1) * Cg, :]
             for i in range(O):
                 row = NB * ROWS + i * HALFJ + j // p.JT
-                c = M[zero[m] + j % p.JT, y + 1, row:row + 1, :]
+                c = M[j % p.JT, y + 1, row:row + 1, :]
                 if i == j:
                     c = c - theta
                 acc[i] = acc[i] + c * v
@@ -441,15 +439,32 @@
     theta = None
     for m in range(ITERS):
         last = m + 1 == ITERS
-        for g in range(NG):
-            if m > 0:
+        if m > 0:
+            for g in range(NG):
                 spread_field(m, range(1, Y + 1), g)
-            for y in range(Y):
-                acc = zeros()
-                if m > 0 and 0 < y < Y - 1:
-                    add_onsite(acc, m, y, theta, g)
-                add_bonds(acc, m, y, [s for s in (-1, 0, 1) if inside(y + s)], g)
-                put(acc, m + 1, y, g)
+
+        def interior(y, steps, g):
+            acc = zeros()
+            if m > 0 and len(steps) == 3:
+                add_onsite(acc, m, y, theta, g)
+            add_bonds(acc, m, y, steps, g)
+            put(acc, m + 1, y, g)
+
+        def middle(q, carry):
+            interior(1 + lax.div(q, NG), (-1, 0, 1), lax.rem(q, NG))
+            return carry
+
+        def first(g, carry):
+            interior(0, (0, 1), g)
+            return carry
+
+        def final(g, carry):
+            interior(Y - 1, (-1, 0), g)
+            return carry
+
+        lax.fori_loop(0, NG, first, 0)
+        lax.fori_loop(0, (Y - 2) * NG, middle, 0)
+        lax.fori_loop(0, NG, final, 0)
         if m == 0:
             moments.append(moment(0, 0))
             theta = take_outer()

time: 37.6 us -> 38.1 us (1.013)
  Pallas kernels: 36.8 us -> 37.3 us
    pallas_call x1, Pallas kernels: 35.7 us -> 36.2 us  [per_device(): pl.pallas_call(functools.partial(kernel, p), out_shape=(scratch(ITERS + 1...]
where the time goes in v8:
time: 38.1 us; the launch traced here: 37.9 us
  Pallas kernels  37.3 us (98%)
  between operations  0.64 us (2%)
    pallas_call x1, Pallas kernels, per_device(): pl.pallas_call(functools.partial(kernel, p), out_shape=(scratch(ITERS + 1...  36.2 us
    pallas_call x1, Pallas kernels, per_device(): pl.pallas_call(functools.partial(combine, p), out_shape=(jax.ShapeDtypeSt...  1.1 us

profile of v8, /device:TPU:0, one launch (start us, length us, event | category | flops | bytes accessed | tf_op | source)
XLA Modules:
  0.0 37.9 jit_solution(14917900324532590008)
XLA Ops:
  0.6 36.2 %shard_map.77 = (f32[4,512,128]{2,1,0:T(8,128)S(1)}, f32[7,8,128]{2,1,0:T(8,128)S(1)}) custom-call(f32[4,4,32,128]{3,2,1,0:T(8,128)} %bitcast.25, f32[1024,13]{1,0:T(8,128)} %bitcast.24, s32[64,13]{1,0:T(8,128)} %bitcast.27, f32[256,4]{1,0:T(8,128)} %bitcast.26, f32[64,4]{1,0:T(8,128)} %bitcast.28, f32[1,256]{1,0:T(1,128)} %bitcast.29), custom_call_target="tpu_custom_call" | custom-call | tf_op jit(solution)/shard_map/pallas_call | solution.py:618
  36.8 1.1 %shard_map.78 = (f32[4,4,32,128]{3,2,1,0:T(8,128)}, f32[4,4,32,128]{3,2,1,0:T(8,128)}) custom-call(f32[4,512,128]{2,1,0:T(8,128)S(1)} %get-tuple-element.6.BT, f32[7,8,128]{2,1,0:T(8,128)S(1)} %get-tuple-element.7.FX), custom_call_target="tpu_custom_call" | custom-call | tf_op jit(solution)/shard_map/pallas_call | solution.py:661

commit v9 on v8

--- a/solution.py
+++ b/solution.py
@@ -393,6 +393,7 @@
             sums.append(jnp.sum(total, axis=1, keepdims=True))
         return jnp.concatenate(sums, axis=0)
 
+    nils = [lax.div(ax, p.nx), lax.div(ay, p.ny), lax.div(az, p.nz), lax.div(me, S)]
     moments = []
     home_copies = {}
 
@@ -450,21 +451,9 @@
             add_bonds(acc, m, y, steps, g)
             put(acc, m + 1, y, g)
 
-        def middle(q, carry):
-            interior(1 + lax.div(q, NG), (-1, 0, 1), lax.rem(q, NG))
-            return carry
-
-        def first(g, carry):
-            interior(0, (0, 1), g)
-            return carry
-
-        def final(g, carry):
-            interior(Y - 1, (-1, 0), g)
-            return carry
-
-        lax.fori_loop(0, NG, first, 0)
-        lax.fori_loop(0, (Y - 2) * NG, middle, 0)
-        lax.fori_loop(0, NG, final, 0)
+        for g in range(NG):
+            for y in range(Y):
+                interior(y, [n for n in (-1, 0, 1) if inside(y + n)], g + nils[y])
         if m == 0:
             moments.append(moment(0, 0))
             theta = take_outer()

time: 38.1 us -> 37.6 us (0.987)
  Pallas kernels: 37.3 us -> 36.8 us
    pallas_call x1, Pallas kernels: 36.2 us -> 35.6 us  [per_device(): pl.pallas_call(functools.partial(kernel, p), out_shape=(scratch(ITERS + 1...]
where the time goes in v9:
time: 37.6 us; the launch traced here: 37.4 us
  Pallas kernels  36.8 us (98%)
  between operations  0.64 us (2%)
    pallas_call x1, Pallas kernels, per_device(): pl.pallas_call(functools.partial(kernel, p), out_shape=(scratch(ITERS + 1...  35.6 us
    pallas_call x1, Pallas kernels, per_device(): pl.pallas_call(functools.partial(combine, p), out_shape=(jax.ShapeDtypeSt...  1.1 us

profile of v9, /device:TPU:0, one launch (start us, length us, event | category | flops | bytes accessed | tf_op | source)
XLA Modules:
  0.0 37.4 jit_solution(2749121944201849996)
XLA Ops:
  0.6 35.6 %shard_map.77 = (f32[4,512,128]{2,1,0:T(8,128)S(1)}, f32[7,8,128]{2,1,0:T(8,128)S(1)}) custom-call(f32[4,4,32,128]{3,2,1,0:T(8,128)} %bitcast.25, f32[1024,13]{1,0:T(8,128)} %bitcast.24, s32[64,13]{1,0:T(8,128)} %bitcast.27, f32[256,4]{1,0:T(8,128)} %bitcast.26, f32[64,4]{1,0:T(8,128)} %bitcast.28, f32[1,256]{1,0:T(1,128)} %bitcast.29), custom_call_target="tpu_custom_call" | custom-call | tf_op jit(solution)/shard_map/pallas_call | solution.py:607
  36.3 1.1 %shard_map.78 = (f32[4,4,32,128]{3,2,1,0:T(8,128)}, f32[4,4,32,128]{3,2,1,0:T(8,128)}) custom-call(f32[4,512,128]{2,1,0:T(8,128)S(1)} %get-tuple-element.6.BT, f32[7,8,128]{2,1,0:T(8,128)S(1)} %get-tuple-element.7.FX), custom_call_target="tpu_custom_call" | custom-call | tf_op jit(solution)/shard_map/pallas_call | solution.py:650
